TPU v7x, 128 devices: a whole 4x4x4 slice. The times are simulated.
128 devices in a mesh: head: 4 (over y_hi, core), seq: 32 (over x, z, y_lo).
Axes of the slice: x: 4, y: 4 (y_hi: 2, y_lo: 2; y = y_hi * 2 + y_lo), z: 4, core: 2. Of those that a mesh axis runs over, the one named last changes fastest.
Arguments:
- queries: bfloat16 [32768, 4096], P('seq', 'head'), may hold values from -6 to 6
- keys: bfloat16 [32768, 512], P('seq', 'head'), may hold values from -6 to 6
- values: bfloat16 [32768, 512], P('seq', 'head'), may hold values from -6 to 6
- vertical: int32 [32, 8], P('head'), may hold values from 0 to 255, as said below
- slash: int32 [32, 8], P('head'), may hold values from 1 to 28, as said below
Outputs:
- attended: bfloat16 [32768, 4096], P(('seq', 'head'))
Inputs may be any that keep to these rules, and one draw needn't show every extreme that they name: `vertical`: each row names 8 different blocks. Within each group of 8 consecutive rows, the different blocks named that lie in one slab (blocks s * 8 to s * 8 + 7) number at most 4, and exactly 4 in some slab. `slash`: each row names 8 different offsets.
All inputs are finite; a program needn't handle non-finite values.
Results may differ from a plain program's by a relative error of at most 0.0033.
Values may be sent and summed in bfloat16 or wider, within the bound.
A program may use at most 128 MiB of HBM per device.

v0:
```python
import math

import jax
import jax.numpy as jnp
from jax import lax
from jax.sharding import Mesh
from jax.sharding import PartitionSpec as P

BLK = 128
LARGEST_OFFSET = 28
CAP = 4
SEQ = ("seq_0", "seq_1", "seq_2")
SEQ_HEAD = ("seq_0", "seq_1", "seq_2", "head")


NEG = -1e30


def joined_along(blocks, dim):
    dims = list(blocks.shape[1:])
    dims[dim] *= blocks.shape[0]
    return jnp.moveaxis(blocks, 0, dim).reshape(dims)


def stacked_from(array, axes, order):
    blocks = array
    for k in order:
        blocks = lax.all_gather(blocks, axes[k])
    done = order[::-1]
    back = [done.index(k) for k in range(len(axes))]
    blocks = blocks.transpose(*back, *range(len(axes), blocks.ndim))
    return blocks.reshape(-1, *array.shape)


def whole_of(array, axes, order, dim):
    return joined_along(stacked_from(array, axes, order), dim)


def shifted(array, axis, by):
    peers = lax.axis_size(axis)
    pairs = [(i, i + by) for i in range(peers) if 0 <= i + by < peers]
    return lax.ppermute(array, axis, pairs)


def attend(query_block, diag_kv, slash_parts, column_kv, slash_ok, column_ok):
    block_count, block_width, head_width = query_block.shape
    score_scale = 1.0 / math.sqrt(head_width)
    causal = jnp.arange(block_width)[:, None] >= jnp.arange(block_width)[None, :]
    diag_scores = (
        jnp.einsum(
            "ird,icd->irc",
            query_block,
            diag_kv[..., :head_width],
            preferred_element_type=jnp.float32,
        )
        * score_scale
    )
    diag_scores = jnp.where(causal[None], diag_scores, NEG)
    slash_scores = []
    for number, part_kv in enumerate(slash_parts):
        part_scores = (
            jnp.einsum(
                "ird,icd->irc",
                query_block,
                part_kv[..., :head_width],
                preferred_element_type=jnp.float32,
            )
            * score_scale
        )
        slash_scores.append(jnp.where(slash_ok[:, number, None, None], part_scores, NEG))
    column_scores = (
        jnp.einsum(
            "ird,jcd->irjc",
            query_block,
            column_kv[..., :head_width],
            preferred_element_type=jnp.float32,
        )
        * score_scale
    )
    column_scores = jnp.where(column_ok[:, None, :, None], column_scores, NEG)
    row_top = jnp.maximum(jnp.max(diag_scores, axis=2), jnp.max(column_scores, axis=(2, 3)))
    for part_scores in slash_scores:
        row_top = jnp.maximum(row_top, jnp.max(part_scores, axis=2))
    diag_weights = jnp.exp(diag_scores - row_top[:, :, None])
    column_weights = jnp.exp(column_scores - row_top[:, :, None, None])
    row_total = jnp.sum(diag_weights, axis=2) + jnp.sum(column_weights, axis=(2, 3))
    mixed_sum = jnp.einsum(
        "irc,icd->ird",
        diag_weights.astype(jnp.bfloat16),
        diag_kv[..., head_width:],
        preferred_element_type=jnp.float32,
    )
    mixed_sum = mixed_sum + jnp.einsum(
        "irjc,jcd->ird",
        column_weights.astype(jnp.bfloat16),
        column_kv[..., head_width:],
        preferred_element_type=jnp.float32,
    )
    for part_scores, part_kv in zip(slash_scores, slash_parts):
        part_weights = jnp.exp(part_scores - row_top[:, :, None])
        row_total = row_total + jnp.sum(part_weights, axis=2)
        mixed_sum = mixed_sum + jnp.einsum(
            "irc,icd->ird",
            part_weights.astype(jnp.bfloat16),
            part_kv[..., head_width:],
            preferred_element_type=jnp.float32,
        )
    return (mixed_sum / row_total[:, :, None]).astype(jnp.bfloat16)


def shards(queries, keys, values, vertical, slash):
    head_width = keys.shape[1]
    slab_rows = queries.shape[0]
    slab_blocks = slab_rows // BLK
    group_heads = vertical.shape[0]
    column_count = vertical.shape[1]
    slash_count = slash.shape[1]
    reach = (LARGEST_OFFSET + slab_blocks - 1) // slab_blocks
    slab_index = lax.axis_index(SEQ)
    local_kv = jnp.concatenate([keys, values], axis=1)
    flat_columns = vertical.reshape(-1)
    block_ids = slab_index * slab_blocks + jnp.arange(slab_blocks, dtype=jnp.int32)
    used = jnp.any(flat_columns[:, None] == block_ids[None, :], axis=0)
    ranks = jnp.cumsum(used.astype(jnp.int32)) - 1
    select = used[None, :] & (ranks[None, :] == jnp.arange(CAP, dtype=jnp.int32)[:, None])
    packed = jnp.dot(
        select.astype(jnp.bfloat16),
        local_kv.reshape(slab_blocks, BLK * 2 * head_width),
        preferred_element_type=jnp.float32,
    )
    packed = packed.astype(jnp.bfloat16).reshape(CAP, BLK, 2 * head_width)
    packed_ids = jnp.where(
        jnp.any(select, axis=1), jnp.sum(jnp.where(select, block_ids[None, :], 0), axis=1), -1
    )
    all_packed, all_ids = (
        whole_of(packed, SEQ, (2, 0, 1), 0),
        whole_of(packed_ids, SEQ, (2, 0, 1), 0),
    )
    slot_ids = jnp.arange(all_ids.shape[0], dtype=jnp.int32)
    position = jnp.sum(
        jnp.where(all_ids[None, :] == flat_columns[:, None], slot_ids[None, :], 0), axis=1
    )
    column_kv = jnp.take(all_packed, position, axis=0).reshape(
        group_heads, column_count, BLK, 2 * head_width
    )
    earlier_parts = [shifted(local_kv, SEQ, step_back) for step_back in range(reach, 0, -1)]
    extended = jnp.concatenate(earlier_parts + [local_kv], axis=0)
    extended_blocks = extended.reshape(-1, BLK, 2 * head_width)
    base_block = reach * slab_blocks
    diag_kv = extended_blocks[base_block : base_block + slab_blocks]
    local_ids = jnp.arange(slab_blocks, dtype=jnp.int32)
    global_ids = slab_index * slab_blocks + local_ids

    def one_head(head_index, attended):
        query_block = lax.dynamic_slice_in_dim(
            queries, head_index * head_width, head_width, 1
        ).reshape(slab_blocks, BLK, head_width)
        offsets = lax.dynamic_index_in_dim(slash, head_index, 0, keepdims=False)
        columns = lax.dynamic_index_in_dim(vertical, head_index, 0, keepdims=False)
        head_kv = lax.dynamic_index_in_dim(column_kv, head_index, 0, keepdims=False)
        slash_parts = [
            lax.dynamic_slice_in_dim(extended_blocks, base_block - offsets[number], slab_blocks, 0)
            for number in range(slash_count)
        ]
        slash_ok = global_ids[:, None] - offsets[None, :] >= 0
        covered = jnp.any(
            global_ids[:, None, None] - columns[None, :, None] == offsets[None, None, :], axis=2
        )
        column_ok = (columns[None, :] < global_ids[:, None]) & jnp.logical_not(covered)
        result = attend(query_block, diag_kv, slash_parts, head_kv, slash_ok, column_ok)
        return lax.dynamic_update_slice_in_dim(
            attended, result.reshape(slab_rows, head_width), head_index * head_width, 1
        )

    attended = lax.fori_loop(
        0, group_heads, one_head, jnp.zeros((slab_rows, group_heads * head_width), jnp.bfloat16)
    )
    return lax.all_to_all(attended, "head", split_axis=0, concat_axis=1, tiled=True)


def solution(mesh):
    split = Mesh(
        mesh.devices.reshape(mesh.shape["head"], 4, 4, 2), ("head", "seq_0", "seq_1", "seq_2")
    )
    return jax.shard_map(
        shards,
        mesh=split,
        in_specs=(P(SEQ, "head"), P(SEQ, "head"), P(SEQ, "head"), P("head", None), P("head", None)),
        out_specs=P(SEQ_HEAD, None),
        check_vma=False,
    )
```

profile of v0, /device:TPU:7, one launch (start us, length us, event | category | flops | bytes accessed | tf_op | source)
XLA Modules:
  0.0 641.6 jit_solution(3345484150491283978)
XLA Ops:
  12.7 8.0 %all_gather.36 = bf16[2,4,128,256]{3,2,1,0:T(8,128)(2,1)} all-gather(bf16[1,4,128,256]{3,2,1,0:T(8,128)(2,1)S(1)} %copy.129), channel_id=1, replica_groups=mesh['head'=4,'seq_0'=4,'seq_1'=4,'seq_2'=2] {'seq_2'}, dimensions={0}, use_global_device_ids=true | all-gather | bytes 786432 | tf_op jit(solution)/shard_map/all_gather | solution.py:28
  20.7 32.0 %all-gather.9.cloned.1.call-done = bf16[8,4,128,256]{3,2,1,0:T(8,128)(2,1)} async-done(((bf16[2,4,128,256]{3,2,1,0:T(8,128)(2,1)}), bf16[8,4,128,256]{3,2,1,0:T(8,128)(2,1)}) %all-gather.9.cloned.1.call-update) | async-done | bytes 2097168 | tf_op jit(solution)/shard_map/all_gather | solution.py:28
  52.8 4.9 collective-permute-start
  57.7 3.2 collective-permute-start.1
  64.4 7.7 %all-reduce = s32[8]{0:T(128)S(1)} all-reduce(s32[8]{0:T(128)S(1)} %select_dynamic-update-slice_fusion), channel_id=2, replica_groups=mesh['head'=4,'seq_0'=4,'seq_1'=4,'seq_2'=2] {'seq_2'}, use_global_device_ids=true, to_apply=%add | all-reduce | flops 8 | bytes 64
  72.2 3.5 collective-permute-start.3
  75.7 8.5 %all-gather.5 = s32[4,2,4]{2,1,0:T(2,128)S(1)} all-gather(s32[1,2,4]{2,1,0:T(2,128)S(1)} %reshape.453), channel_id=3, replica_groups=mesh['head'=4,'seq_0'=4,'seq_1'=4,'seq_2'=2] {'seq_0'}, dimensions={0}, use_global_device_ids=true | all-gather | bytes 160 | tf_op jit(solution)/shard_map/all_gather | solution.py:28
  84.3 40.6 %all-gather.2 = s32[16,2,4]{2,1,0:T(2,128)S(1)} all-gather(s32[4,2,4]{2,1,0:T(2,128)S(1)} %all-gather.5), channel_id=4, replica_groups=mesh['head'=4,'seq_0'=4,'seq_1'=4,'seq_2'=2] {'seq_1'}, dimensions={0}, use_global_device_ids=true | all-gather | bytes 640 | tf_op jit(solution)/shard_map/all_gather | solution.py:28
  130.2 43.3 %all-gather.11.cloned.1.call-done = bf16[16,2,4,128,256]{4,3,2,1,0:T(8,128)(2,1)} async-done(((bf16[4,2,4,128,256]{4,3,2,1,0:T(8,128)(2,1)}), bf16[16,2,4,128,256]{4,3,2,1,0:T(8,128)(2,1)}) %all-gather.11.cloned.1.call-update) | async-done | bytes 8388624 | tf_op jit(solution)/shard_map/all_gather | solution.py:28
  173.4 7.7 %copy.111 = bf16[4,4,2,4,128,256]{5,4,3,2,1,0:T(8,128)(2,1)} copy(bf16[4,4,2,4,128,256]{5,4,3,2,0,1:T(8,128)(2,1)} %bitcast.161) | data formatting | bytes 16777216 | tf_op jit(solution)/shard_map/transpose | solution.py:31
  181.1 6.2 gather_fusion
  187.3 4.5 broadcast_select_fusion
  193.4 403.4 %while.17 = (s32[]{:T(128)}, bf16[1024,1024]{1,0:T(8,128)(2,1)}, bf16[1024,1024]{1,0:T(8,128)(2,1)}, bf16[8,128,256]{2,1,0:T(8,128)(2,1)}, s32[8,8]{1,0:T(8,128)...) while((s32[]{:T(128)}, bf16[1024,1024]{1,0:T(8,128)(2,1)}, ...), condition=%wide.region_27.28_spmd.clone, body=%wide.region_5.27_spmd.clone.sunk | while | flops 1162099968 | bytes 94896152 | solution.py:175
  198.2 2.7 fusion.199
  215.1 2.1 fusion.205
  218.5 2.1 fusion.206
  225.2 2.1 fusion.208
  228.6 3.9 fusion.210
  232.6 2.1 convolution_add_fusion.17
  248.6 2.7 fusion.199
  265.5 2.1 fusion.205
  269.0 2.1 fusion.206
  275.7 2.1 fusion.208
  279.1 3.9 fusion.210
  283.0 2.1 convolution_add_fusion.17
  299.0 2.7 fusion.199
  316.0 2.1 fusion.205
  319.4 2.1 fusion.206
  326.1 2.1 fusion.208
  329.5 3.9 fusion.210
  333.4 2.1 convolution_add_fusion.17
  349.4 2.7 fusion.199
  366.4 2.1 fusion.205
  369.8 2.1 fusion.206
  376.5 2.1 fusion.208
  379.9 3.9 fusion.210
  383.8 2.1 convolution_add_fusion.17
  399.9 2.7 fusion.199
  416.8 2.1 fusion.205
  420.2 2.1 fusion.206
  426.9 2.1 fusion.208
  430.3 3.9 fusion.210
  434.3 2.1 convolution_add_fusion.17
  450.3 2.7 fusion.199
  467.2 2.1 fusion.205
  470.7 2.1 fusion.206
  477.4 2.1 fusion.208
  480.8 3.9 fusion.210
  484.7 2.1 convolution_add_fusion.17
  500.7 2.7 fusion.199
  517.7 2.1 fusion.205
  521.1 2.1 fusion.206
  527.8 2.1 fusion.208
  531.2 3.9 fusion.210
  535.1 2.1 convolution_add_fusion.17
  551.1 2.7 fusion.199
  568.1 2.1 fusion.205
  571.5 2.1 fusion.206
  578.2 2.1 fusion.208
  581.6 3.9 fusion.210
  585.5 2.1 convolution_add_fusion.17
  596.8 31.3 %all_to_all.19 = bf16[4,256,1024]{2,1,0:T(8,128)(2,1)S(1)} all-to-all(bf16[4,256,1024]{2,1,0:T(8,128)(2,1)} %bitcast.162), channel_id=1, replica_groups=mesh['head'=4,'seq_0'=4,'seq_1'=4,'seq_2'=2] {'head'}, dimensions={0} | all-to-all | bytes 4194304 | tf_op jit(solution)/shard_map/all_to_all | solution.py:178
  628.1 2.6 copy.112
  630.7 4.1 copy.113
  (489 shorter events, 218.4 us)
Async XLA Ops:
  6.5 46.2 %all-gather.9.cloned.1.call-start = ((), (), s32[]{:S(2)}) async-start(), calls=%async_computation.1 | async-start | bytes 2621440 | tf_op jit(solution)/shard_map/all_gather | solution.py:28
  11.2 49.7 %copy-start.15 = (u32[128]{0:T(128)S(1)}, u32[128]{0:T(128)}, u32[]{:S(2)}) copy-start(u32[128]{0:T(128)} %constant.207) | copy-start | bytes 1540
  20.7 152.8 %all-gather.11.cloned.1.call-start = ((), (), s32[]{:S(2)}) async-start(), calls=%async_computation.2 | async-start | bytes 10485760 | tf_op jit(solution)/shard_map/all_gather | solution.py:28
  52.8 77.2 %copy-start.13 = (bf16[1024,128]{1,0:T(8,128)(2,1)S(1)}, bf16[1024,128]{1,0:T(8,128)(2,1)}, u32[]{:S(2)}) copy-start(bf16[1024,128]{1,0:T(8,128)(2,1)} %param.8) | copy-start | bytes 786436
  52.8 77.3 %copy-start.14 = (bf16[1024,128]{1,0:T(8,128)(2,1)S(1)}, bf16[1024,128]{1,0:T(8,128)(2,1)}, u32[]{:S(2)}) copy-start(bf16[1024,128]{1,0:T(8,128)(2,1)} %param.9) | copy-start | bytes 786436
  52.8 72.8 %collective-permute-start = (bf16[1024,256]{1,0:T(8,128)(2,1)}, bf16[1024,256]{1,0:T(8,128)(2,1)}, u32[]{:S(2)}, u32[]{:S(2)}) collective-permute-start(bf16[1024,256]{1,0:T(8,128)(2,1)} %constant_dynamic-update-slice_fusion.1), channel_id=1, source_target_pairs={{0,4},{1,5},{2,6},{3,7},{4,8},{5,9},{6,10},{7,11},{8,12},{9,13},{1... | collective-permute-start | bytes 1572872 | tf_op jit(solution)/shard_map/ppermute | solution.py:42
  57.7 69.0 %collective-permute-start.1 = (bf16[1024,256]{1,0:T(8,128)(2,1)}, bf16[1024,256]{1,0:T(8,128)(2,1)}, u32[]{:S(2)}, u32[]{:S(2)}) collective-permute-start(bf16[1024,256]{1,0:T(8,128)(2,1)} %constant_dynamic-update-slice_fusion.1), channel_id=1, source_target_pairs={{0,3},{1,4},{2,5},{3,6},{4,7},{5,8},{6,9},{7,10},{8,11},{9,12},{10... | collective-permute-start | bytes 1572872 | tf_op jit(solution)/shard_map/ppermute | solution.py:42
  62.5 65.3 %collective-permute-start.2 = (bf16[1024,256]{1,0:T(8,128)(2,1)}, bf16[1024,256]{1,0:T(8,128)(2,1)}, u32[]{:S(2)}, u32[]{:S(2)}) collective-permute-start(bf16[1024,256]{1,0:T(8,128)(2,1)} %constant_dynamic-update-slice_fusion.1), channel_id=1, source_target_pairs={{0,2},{1,3},{2,4},{3,5},{4,6},{5,7},{6,8},{7,9},{8,10},{9,11},{10,... | collective-permute-start | bytes 1572872 | tf_op jit(solution)/shard_map/ppermute | solution.py:42
  72.2 56.7 %collective-permute-start.3 = (bf16[1024,256]{1,0:T(8,128)(2,1)}, bf16[1024,256]{1,0:T(8,128)(2,1)}, u32[]{:S(2)}, u32[]{:S(2)}) collective-permute-start(bf16[1024,256]{1,0:T(8,128)(2,1)} %constant_dynamic-update-slice_fusion.1), channel_id=1, source_target_pairs={{0,1},{1,2},{2,3},{3,4},{4,5},{5,6},{6,7},{7,8},{8,9},{9,10},{10,1... | collective-permute-start | bytes 1572872 | tf_op jit(solution)/shard_map/ppermute | solution.py:42
  130.2 51.0 %copy-start.1 = (bf16[5120,256]{1,0:T(8,128)(2,1)}, bf16[5120,256]{1,0:T(8,128)(2,1)S(1)}, u32[]{:S(2)}) copy-start(bf16[5120,256]{1,0:T(8,128)(2,1)S(1)} %constant_dynamic-update-slice_fusion.8) | copy-start | bytes 7864324
  198.2 5.5 copy-start.2
  228.6 3.9 copy-start.10
  234.6 3.0 copy-start.6
  234.7 3.3 copy-start.5
  236.2 2.0 copy-start.4
  238.3 1.5 copy-start.11
  239.3 2.3 copy-start
  248.6 5.5 copy-start.2
  279.0 3.9 copy-start.10
  285.1 3.0 copy-start.6
  285.1 3.3 copy-start.5
  286.7 2.0 copy-start.4
  288.7 1.5 copy-start.11
  289.7 2.3 copy-start
  299.0 5.5 copy-start.2
  329.5 3.9 copy-start.10
  335.5 3.0 copy-start.6
  335.5 3.3 copy-start.5
  337.1 2.0 copy-start.4
  339.2 1.5 copy-start.11
  340.1 2.3 copy-start
  349.4 5.5 copy-start.2
  379.9 3.9 copy-start.10
  385.9 3.0 copy-start.6
  385.9 3.3 copy-start.5
  387.5 2.0 copy-start.4
  389.6 1.5 copy-start.11
  390.6 2.3 copy-start
  399.9 5.5 copy-start.2
  430.3 3.9 copy-start.10
  436.3 3.0 copy-start.6
  436.4 3.3 copy-start.5
  437.9 2.0 copy-start.4
  440.0 1.5 copy-start.11
  441.0 2.3 copy-start
  450.3 5.5 copy-start.2
  480.7 3.9 copy-start.10
  486.8 3.0 copy-start.6
  486.8 3.3 copy-start.5
  488.4 2.0 copy-start.4
  490.4 1.5 copy-start.11
  491.4 2.3 copy-start
  500.7 5.5 copy-start.2
  531.2 3.9 copy-start.10
  537.2 3.0 copy-start.6
  537.2 3.3 copy-start.5
  538.8 2.0 copy-start.4
  541.8 2.3 copy-start
  551.1 5.5 copy-start.2
  581.6 3.9 copy-start.10
  587.6 3.0 copy-start.6
  587.6 3.3 copy-start.5
  589.2 2.0 copy-start.4
  592.3 2.3 copy-start
  (42 other events, 47.7 us)
Sparse Core Ops, SparseCore 0:
  20.8 31.8 all-gather.8
  54.4 118.9 all-gather.10
where the time goes:
time: 649 us; the launch traced here: 642 us
  matrix products  237 us (37%)
  local copies, waits for them, and re-layouts  96.1 us (15%)
  blocking collectives  96.1 us (15%)
  loops' own time  81.6 us (13%)
  waiting for transfers between devices  75.3 us (12%)
  other arithmetic  28 us (4%)
  between operations  14.3 us (2%)
  starting transfers between devices  13.6 us (2%)
    dot_general x64, matrix products, attend(): jnp.einsum('ird,icd->irc', query_block, part_kv[..., :head_width], prefer...  118 us
    another operation x1, loops' own time, shards(): lax.fori_loop(0, group_heads, one_head, jnp.zeros((slab_rows, group_heads...  81.6 us
    all_gather x2, waiting for transfers between devices, stacked_from(): blocks = lax.all_gather(blocks, axes[k])  75.3 us
    all_gather x3, blocking collectives, stacked_from(): blocks = lax.all_gather(blocks, axes[k])  57.1 us
    dot_general x64, matrix products, attend(): jnp.einsum('irc,icd->ird', part_weights.astype(jnp.bfloat16), part_kv[......  38.3 us
    all_to_all x1, blocking collectives, shards(): lax.all_to_all(attended, 'head', split_axis=0, concat_axis=1, tiled=True)  31.3 us
    dot_general x8, matrix products, attend(): jnp.einsum('irjc,jcd->ird', column_weights.astype(jnp.bfloat16), column_k...  31.2 us
    dot_general x8, matrix products, attend(): jnp.einsum('ird,jcd->irjc', query_block, column_kv[..., :head_width], pre...  21.5 us
  transfers between devices with their start and end apart: 6, of which 2 were waited for; matrix products, arithmetic and copies ran while one was open for 1% of the time, Pallas kernels for 0%

commit v1 on v0

v1 whole, which is shorter than its diff:
```python
import functools, math
import jax, jax.numpy as jnp
from jax import lax
from jax.experimental import pallas as pl
from jax.experimental.pallas import tpu as pltpu
from jax.sharding import Mesh
from jax.sharding import PartitionSpec as P

BLK = 128
NEG = -1e30
BACK = 28
F32 = jnp.float32
BF16 = jnp.bfloat16
SCALE2 = math.log2(math.e) / math.sqrt(128.0)


def dot(a, b):
    return jnp.dot(a, b, preferred_element_type=F32)


def lane_max(parts):
    top = parts[0]
    for part in parts[1:]:
        top = jnp.maximum(top, part)
    return jnp.max(top, axis=1, keepdims=True)


def lane_sum(parts):
    total = parts[0]
    for part in parts[1:]:
        total = total + part
    return jnp.sum(total, axis=1, keepdims=True)


def near_step(h, i, slab, slash_ref, q_ref, ext_ref, acc_ref, top_ref, sum_ref):
    rows = pl.ds(pl.multiple_of(i * BLK, BLK), BLK)
    q = q_ref[h, rows, :]
    row = lax.broadcasted_iota(jnp.int32, (BLK, BLK), 0)
    col = lax.broadcasted_iota(jnp.int32, (BLK, BLK), 1)
    own = BACK + i
    scores = [jnp.where(row >= col, dot(q, ext_ref[own, 0]), NEG)]
    blocks = [own]
    for n in range(0, 8, 2):
        pair, bias = [], []
        for k in (n, n + 1):
            off = slash_ref[h, k]
            ok = slab * 8 + i - off >= 0
            pair.append(jnp.where(ok, own - off, own))
            bias.append(jnp.where(ok, 0.0, NEG).astype(F32))
        both = dot(q, jnp.concatenate([ext_ref[pair[0], 0], ext_ref[pair[1], 0]], axis=1))
        scores.append(both[:, :BLK] + bias[0])
        scores.append(both[:, BLK:] + bias[1])
        blocks += pair
    top = lane_max(scores)
    weights = [jnp.exp2((s - top) * SCALE2) for s in scores]
    acc = dot(weights[0].astype(BF16), ext_ref[blocks[0], 1])
    for n in range(1, 9, 2):
        p = jnp.concatenate([weights[n].astype(BF16), weights[n + 1].astype(BF16)], axis=1)
        v = jnp.concatenate([ext_ref[blocks[n], 1], ext_ref[blocks[n + 1], 1]], axis=0)
        acc = acc + dot(p, v)
    acc_ref[h, rows, :] = acc
    top_ref[h, rows, :] = top
    sum_ref[h, rows, :] = lane_sum(weights)


def far_step(h, i, slab, slash_ref, vert_ref, pos_ref, q_ref, far_ref, acc_ref, top_ref, sum_ref, out_ref):
    rows = pl.ds(pl.multiple_of(i * BLK, BLK), BLK)
    q = q_ref[h, rows, :]
    mine = slab * 8 + i
    bias, places = [], []
    for k in range(8):
        name = vert_ref[h, k]
        gap = mine - name
        ok = gap > 0
        for n in range(8):
            ok = ok & (slash_ref[h, n] != gap)
        bias.append(jnp.where(ok, 0.0, NEG).astype(F32))
        places.append(pos_ref[h, k])
    scores = []
    for k in range(0, 8, 2):
        both = dot(q, jnp.concatenate([far_ref[places[k], 0], far_ref[places[k + 1], 0]], axis=1))
        scores.append(both[:, :BLK] + bias[k])
        scores.append(both[:, BLK:] + bias[k + 1])
    old = top_ref[h, rows, :]
    top = jnp.maximum(old, lane_max(scores))
    keep = jnp.exp2((old - top) * SCALE2)
    weights = [jnp.exp2((s - top) * SCALE2) for s in scores]
    acc = None
    for k in range(0, 8, 2):
        p = jnp.concatenate([weights[k].astype(BF16), weights[k + 1].astype(BF16)], axis=1)
        v = jnp.concatenate([far_ref[places[k], 1], far_ref[places[k + 1], 1]], axis=0)
        acc = dot(p, v) if acc is None else acc + dot(p, v)
    total = sum_ref[h, rows, :] * keep + lane_sum(weights)
    out_ref[h, rows, :] = ((acc_ref[h, rows, :] * keep + acc) / total).astype(BF16)


CAP = 4
SEQ = ("seq_0", "seq_1", "seq_2")
SEQ_HEAD = ("seq_0", "seq_1", "seq_2", "head")
UNROLL = 4


def joined_along(blocks, dim):
    dims = list(blocks.shape[1:])
    dims[dim] *= blocks.shape[0]
    return jnp.moveaxis(blocks, 0, dim).reshape(dims)


def stacked_from(array, axes, order):
    blocks = array
    for k in order:
        blocks = lax.all_gather(blocks, axes[k])
    done = order[::-1]
    back = [done.index(k) for k in range(len(axes))]
    blocks = blocks.transpose(*back, *range(len(axes), blocks.ndim))
    return blocks.reshape(-1, *array.shape)


def whole_of(array, axes, order, dim):
    return joined_along(stacked_from(array, axes, order), dim)


def shifted(array, axis, by):
    peers = lax.axis_size(axis)
    pairs = [(i, i + by) for i in range(peers) if 0 <= i + by < peers]
    return lax.ppermute(array, axis, pairs)


def kernel(slab_ref, slash, vert, pos, q_hbm, ext_hbm, far_hbm, out_hbm, q, ext, far, acc, top, tot, out, sem):
    loads = [
        pltpu.make_async_copy(q_hbm.at[:, pl.ds(h * 128, 128)], q.at[h], sem.at[h]) for h in range(8)
    ]
    loads.append(pltpu.make_async_copy(ext_hbm, ext, sem.at[8]))
    late = pltpu.make_async_copy(far_hbm, far, sem.at[9])
    for load in loads:
        load.start()
    late.start()
    for load in loads:
        load.wait()
    slab = slab_ref[0]

    @pl.loop(0, 64 // UNROLL)
    def _(t):
        for u in range(UNROLL):
            e = t * UNROLL + u
            near_step(e // 8, e % 8, slab, slash, q, ext, acc, top, tot)

    late.wait()

    @pl.loop(0, 64 // UNROLL)
    def _(t):
        for u in range(UNROLL):
            e = t * UNROLL + u
            far_step(e // 8, e % 8, slab, slash, vert, pos, q, far, acc, top, tot, out)

    stores = [
        pltpu.make_async_copy(out.at[h], out_hbm.at[:, pl.ds(h * 128, 128)], sem.at[h]) for h in range(8)
    ]
    for store in stores:
        store.start()
    for store in stores:
        store.wait()


def attention(slab, slash, vert, pos, q, ext, far):
    whole = pl.BlockSpec(memory_space=pl.ANY)
    scalars = pl.BlockSpec(memory_space=pltpu.SMEM)
    return pl.pallas_call(
        kernel,
        out_shape=jax.ShapeDtypeStruct((1024, 1024), BF16),
        in_specs=[scalars] * 4 + [whole] * 3,
        out_specs=whole,
        scratch_shapes=[
            pltpu.VMEM((8, 1024, 128), BF16),
            pltpu.VMEM((36, 2, 128, 128), BF16),
            pltpu.VMEM((128, 2, 128, 128), BF16),
            pltpu.VMEM((8, 1024, 128), F32),
            pltpu.VMEM((8, 1024, 1), F32),
            pltpu.VMEM((8, 1024, 1), F32),
            pltpu.VMEM((8, 1024, 128), BF16),
            pltpu.SemaphoreType.DMA((10,)),
        ],
        compiler_params=pltpu.CompilerParams(vmem_limit_bytes=60 * 2**20),
    )(slab, slash, vert, pos, q, ext, far)


def shards(queries, keys, values, vertical, slash):
    slab = lax.axis_index(SEQ)
    local_kv = jnp.stack(
        [keys.reshape(8, BLK, BLK).transpose(0, 2, 1), values.reshape(8, BLK, BLK)], axis=1
    )
    flat = vertical.reshape(-1)
    used = jnp.any(flat[:, None] == jnp.arange(256, dtype=jnp.int32)[None, :], axis=0)
    ids = jnp.arange(256, dtype=jnp.int32)
    earlier = used[None, :] & (ids[None, :] // 8 == flat[:, None] // 8) & (ids[None, :] < flat[:, None])
    pos = (flat // 8) * CAP + jnp.sum(earlier.astype(jnp.int32), axis=1)
    mine = lax.dynamic_slice_in_dim(used, slab * 8, 8)
    ranks = jnp.cumsum(mine.astype(jnp.int32)) - 1
    select = mine[None, :] & (ranks[None, :] == jnp.arange(CAP, dtype=jnp.int32)[:, None])
    which = jnp.sum(jnp.where(select, jnp.arange(8, dtype=jnp.int32)[None, :], 0), axis=1)
    packed = jnp.take(local_kv, which, axis=0)
    far = whole_of(packed, SEQ, (2, 0, 1), 0)
    ext = jnp.concatenate([shifted(local_kv, SEQ, k)[(4 if k == 4 else 0):] for k in (4, 3, 2, 1)] + [local_kv], axis=0)
    attended = attention(slab.reshape(1), slash, vertical, pos.reshape(8, 8), queries, ext, far)
    return lax.all_to_all(attended, "head", split_axis=0, concat_axis=1, tiled=True)


def solution(mesh):
    split = Mesh(
        mesh.devices.reshape(mesh.shape["head"], 4, 4, 2), ("head", "seq_0", "seq_1", "seq_2")
    )
    return jax.shard_map(
        shards,
        mesh=split,
        in_specs=(P(SEQ, "head"), P(SEQ, "head"), P(SEQ, "head"), P("head", None), P("head", None)),
        out_specs=P(SEQ_HEAD, None),
        check_vma=False,
    )
```

time: 649 us -> 285 us (0.44)
  matrix products: 237 us -> 0 us
  loops' own time: 81.6 us -> 0 us
  local copies, waits for them, and re-layouts: 96.1 us -> 18.8 us
  waiting for transfers between devices: 75.3 us -> 138 us
  Pallas kernels: 0 us -> 60.2 us
  blocking collectives: 96.1 us -> 39.2 us
  other arithmetic: 28 us -> 2.49 us
    dot_general x161 -> x0, matrix products: 237 us -> none  [the longest x64 118 us: attend(): jnp.einsum('ird,icd->irc', query_block, part_kv[..., :head_width], prefer...]
    another operation x1 -> x0, loops' own time: 81.6 us -> none  [shards(): lax.fori_loop(0, group_heads, one_head, jnp.zeros((slab_rows, group_heads...]
    pallas_call x0 -> x1, Pallas kernels: none -> 60.2 us  [attention(): pl.pallas_call(kernel, out_shape=jax.ShapeDtypeStruct((1024, 1024), BF16)...]
    ppermute x4, waiting for transfers between devices: 0.01 us -> 52 us  [shifted(): return lax.ppermute(array, axis, pairs)]
    all_gather x3 -> x1, blocking collectives: 57.1 us -> 7.96 us  [stacked_from(): blocks = lax.all_gather(blocks, axes[k])]
    reduce_sum x18 -> x2, other arithmetic: 19 us -> 0.3 us  [the longest x1 0.18 us: shards(): pos = flat // 8 * CAP + jnp.sum(earlier.astype(jnp.int32), axis=1)]
    while x192 -> x0, local copies, waits for them, and re-layouts: 16.5 us -> none
    dynamic_slice x16 -> x0, local copies, waits for them, and re-layouts: 13.3 us -> none  [the longest x8 7.8 us: one_head(): lax.dynamic_slice_in_dim(queries, head_index * head_width, head_width, 1)]
  transfers between devices with their start and end apart: 6 -> 6, of which waited for: 2 -> 4; matrix products, arithmetic and copies ran while one was open for 1% -> 2% of each run, Pallas kernels for 0% -> 0%
where the time goes in v1:
time: 285 us; the launch traced here: 284 us
  waiting for transfers between devices  138 us (48%)
  Pallas kernels  60.2 us (21%)
  blocking collectives  39.2 us (14%)
  local copies, waits for them, and re-layouts  18.8 us (7%)
  between operations  13.6 us (5%)
  starting transfers between devices  12.3 us (4%)
    all_gather x2, waiting for transfers between devices, stacked_from(): blocks = lax.all_gather(blocks, axes[k])  85.5 us
    pallas_call x1, Pallas kernels, attention(): pl.pallas_call(kernel, out_shape=jax.ShapeDtypeStruct((1024, 1024), BF16)...  60.2 us
    ppermute x4, waiting for transfers between devices, shifted(): return lax.ppermute(array, axis, pairs)  52 us
    all_to_all x1, blocking collectives, shards(): lax.all_to_all(attended, 'head', split_axis=0, concat_axis=1, tiled=True)  31.2 us
    ppermute x4, starting transfers between devices, shifted(): return lax.ppermute(array, axis, pairs)  12.2 us
    transpose x1, local copies, waits for them, and re-layouts, stacked_from(): blocks = blocks.transpose(*back, *range(len(axes), blocks.ndim))  10.3 us
    all_gather x1, blocking collectives, stacked_from(): blocks = lax.all_gather(blocks, axes[k])  7.96 us
  transfers between devices with their start and end apart: 6, of which 4 were waited for; matrix products, arithmetic and copies ran while one was open for 2% of the time, Pallas kernels for 0%

profile of v1, /device:TPU:7, one launch (start us, length us, event | category | flops | bytes accessed | tf_op | source)
XLA Modules:
  0.0 284.0 jit_solution(1368067907993152252)
XLA Ops:
  6.5 0.0 all-gather.5.cloned.1.call-start
  6.5 0.8 eq.43
  7.3 0.1 fusion
  7.4 0.1 convert_bitcast_fusion
  7.5 0.2 reduce-window.8
  7.7 0.1 select_reduce_fusion
  7.8 1.1 copy.13
  9.0 1.0 pad_maximum_fusion
  10.0 0.0 copy-start.2
  10.0 0.6 gather_fusion
  10.6 0.1 bitcast_select_fusion
  10.7 8.0 %all_gather.16 = bf16[2,4,2,128,128]{4,3,2,1,0:T(8,128)(2,1)} all-gather(bf16[1,4,2,128,128]{4,3,2,1,0:T(8,128)(2,1)S(1)} %bitcast_select_fusion), channel_id=1, replica_groups=mesh['head'=4,'seq_0'=4,'seq_1'=4,'seq_2'=2] {'seq_2'}, dimensions={0}, use_global_device_ids=true | all-gather | bytes 786432 | tf_op jit(solution)/shard_map/all_gather | solution.py:112
  18.6 0.0 all-gather.5.cloned.1.call-update
  18.7 0.0 all-gather.7.cloned.1.call-start
  18.7 32.0 %all-gather.5.cloned.1.call-done = bf16[8,4,2,128,128]{4,3,2,1,0:T(8,128)(2,1)} async-done(((bf16[2,4,2,128,128]{4,3,2,1,0:T(8,128)(2,1)}), bf16[8,4,2,128,128]{4,3,2,1,0:T(8,128)(2,1)}) %all-gather.5.cloned.1.call-update) | async-done | bytes 2097168 | tf_op jit(solution)/shard_map/all_gather | solution.py:112
  50.7 0.0 all-gather.7.cloned.1.call-update
  50.7 0.0 copy-start.1
  50.8 4.9 %collective-permute-start = (bf16[8,2,128,128]{3,2,1,0:T(8,128)(2,1)S(1)}, bf16[8,2,128,128]{3,2,1,0:T(8,128)(2,1)}, u32[]{:S(2)}, u32[]{:S(2)}) collective-permute-start(bf16[8,2,128,128]{3,2,1,0:T(8,128)(2,1)S(1)} %pad_maximum_fusion), channel_id=1, source_target_pairs={{0,4},{1,5},{2,6},{3,7},{4,8},{5,9},{6,10},{7,11},{8,12},{9,13},{1... | collective-permute-start | bytes 1572872 | tf_op jit(solution)/shard_map/ppermute | solution.py:126
  55.7 3.2 %collective-permute-start.1 = (bf16[8,2,128,128]{3,2,1,0:T(8,128)(2,1)S(1)}, bf16[8,2,128,128]{3,2,1,0:T(8,128)(2,1)}, u32[]{:S(2)}, u32[]{:S(2)}) collective-permute-start(bf16[8,2,128,128]{3,2,1,0:T(8,128)(2,1)S(1)} %pad_maximum_fusion), channel_id=1, source_target_pairs={{0,3},{1,4},{2,5},{3,6},{4,7},{5,8},{6,9},{7,10},{8,11},{9,12},{10... | collective-permute-start | bytes 1572872 | tf_op jit(solution)/shard_map/ppermute | solution.py:126
  58.9 1.9 collective-permute-start.2
  60.8 2.2 collective-permute-start.3
  63.0 0.2 convert_reduce_fusion
  63.2 0.1 reduce_sum.23
  63.3 0.0 copy-done.2
  63.3 0.6 fusion.4.pos
  63.9 31.7 %collective-permute-done = bf16[8,2,128,128]{3,2,1,0:T(8,128)(2,1)} collective-permute-done((bf16[8,2,128,128]{3,2,1,0:T(8,128)(2,1)S(1)}, bf16[8,2,128,128]{3,2,1,0:T(8,128)(2,1)}, u32[]{:S(2)}, u32[]{:S(2)}) %collective-permute-start) | collective-permute-done | bytes 524320 | tf_op jit(solution)/shard_map/ppermute | solution.py:126
  95.6 1.0 slice_dynamic-update-slice_fusion
  96.6 0.0 collective-permute-done.1
  96.6 1.1 constant_dynamic-update-slice_fusion.3
  97.7 20.4 %collective-permute-done.2 = bf16[8,2,128,128]{3,2,1,0:T(8,128)(2,1)} collective-permute-done((bf16[8,2,128,128]{3,2,1,0:T(8,128)(2,1)S(1)}, bf16[8,2,128,128]{3,2,1,0:T(8,128)(2,1)}, u32[]{:S(2)}, u32[]{:S(2)}) %collective-permute-start.2) | collective-permute-done | bytes 524320 | tf_op jit(solution)/shard_map/ppermute | solution.py:126
  118.1 1.1 constant_dynamic-update-slice_fusion.2
  119.2 0.0 collective-permute-done.3
  119.2 1.1 constant_dynamic-update-slice_fusion.1
  120.4 0.0 copy-done.1
  120.4 0.1 constant_dynamic-update-slice_fusion.ext_hbm
  120.5 0.0 copy-start
  120.5 53.4 %all-gather.7.cloned.1.call-done = bf16[16,2,4,2,128,128]{5,4,3,2,1,0:T(8,128)(2,1)} async-done(((bf16[4,2,4,2,128,128]{5,4,3,2,1,0:T(8,128)(2,1)}), bf16[16,2,4,2,128,128]{5,4,3,2,1,0:T(8,128)(2,1)}) %all-gather.7.cloned.1.call-update) | async-done | bytes 8388624 | tf_op jit(solution)/shard_map/all_gather | solution.py:112
  173.9 10.3 %copy.14 = bf16[4,4,2,4,2,128,128]{6,5,4,3,2,1,0:T(8,128)(2,1)} copy(bf16[4,4,2,4,2,128,128]{6,5,4,3,2,0,1:T(8,128)(2,1)} %bitcast.27) | data formatting | bytes 16777216 | tf_op jit(solution)/shard_map/transpose | solution.py:115
  184.2 0.0 copy-done
  184.2 60.2 %shard_map.55 = bf16[1024,1024]{1,0:T(8,128)(2,1)} custom-call(s32[1]{0:T(128)} %bitcast.slab_ref, s32[8,8]{1,0:T(8,128)} %slash.1, s32[8,8]{1,0:T(8,128)} %vert.1, s32[8,8]{1,0:T(8,128)} %fusion.4.pos, bf16[1024,1024]{1,0:T(8,128)(2,1)} %q_hbm.1, bf16[36,2,128,128]{3,2,1,0:T(8,128)(2,1)} %copy-done, bf16[128,2,128,128]{3,2,1,0:T(8,128)(2,1)} %bitcast.25), custom_call_target="tpu_custom_call" | custom-call | tf_op jit(solution)/shard_map/pallas_call | solution.py:168
  244.5 31.2 %all_to_all.19 = bf16[4,256,1024]{2,1,0:T(8,128)(2,1)S(1)} all-to-all(bf16[4,256,1024]{2,1,0:T(8,128)(2,1)} %bitcast.26), channel_id=1, replica_groups=mesh['head'=4,'seq_0'=4,'seq_1'=4,'seq_2'=2] {'head'}, dimensions={0} | all-to-all | bytes 4194304 | tf_op jit(solution)/shard_map/all_to_all | solution.py:205
  275.7 1.5 copy.16
  (6 shorter events, 0.0 us)
Async XLA Ops:
  6.5 44.2 %all-gather.5.cloned.1.call-start = ((), (), s32[]{:S(2)}) async-start(), calls=%async_computation.1 | async-start | bytes 2621440 | tf_op jit(solution)/shard_map/all_gather | solution.py:112
  10.0 53.3 %copy-start.2 = (s32[8,8]{1,0:T(8,128)S(1)}, s32[8,8]{1,0:T(8,128)}, u32[]{:S(2)}) copy-start(s32[8,8]{1,0:T(8,128)} %vert.1) | copy-start | bytes 772
  18.7 155.2 %all-gather.7.cloned.1.call-start = ((), (), s32[]{:S(2)}) async-start(), calls=%async_computation.2 | async-start | bytes 10485760 | tf_op jit(solution)/shard_map/all_gather | solution.py:112
  50.7 69.6 %copy-start.1 = (bf16[1024,128]{1,0:T(8,128)(2,1)S(1)}, bf16[1024,128]{1,0:T(8,128)(2,1)}, u32[]{:S(2)}) copy-start(bf16[1024,128]{1,0:T(8,128)(2,1)} %param.7) | copy-start | bytes 786436
  50.8 44.8 %collective-permute-start = (bf16[8,2,128,128]{3,2,1,0:T(8,128)(2,1)S(1)}, bf16[8,2,128,128]{3,2,1,0:T(8,128)(2,1)}, u32[]{:S(2)}, u32[]{:S(2)}) collective-permute-start(bf16[8,2,128,128]{3,2,1,0:T(8,128)(2,1)S(1)} %pad_maximum_fusion), channel_id=1, source_target_pairs={{0,4},{1,5},{2,6},{3,7},{4,8},{5,9},{6,10},{7,11},{8,12},{9,13},{1... | collective-permute-start | bytes 1572872 | tf_op jit(solution)/shard_map/ppermute | solution.py:126
  55.7 40.9 %collective-permute-start.1 = (bf16[8,2,128,128]{3,2,1,0:T(8,128)(2,1)S(1)}, bf16[8,2,128,128]{3,2,1,0:T(8,128)(2,1)}, u32[]{:S(2)}, u32[]{:S(2)}) collective-permute-start(bf16[8,2,128,128]{3,2,1,0:T(8,128)(2,1)S(1)} %pad_maximum_fusion), channel_id=1, source_target_pairs={{0,3},{1,4},{2,5},{3,6},{4,7},{5,8},{6,9},{7,10},{8,11},{9,12},{10... | collective-permute-start | bytes 1572872 | tf_op jit(solution)/shard_map/ppermute | solution.py:126
  58.9 59.2 %collective-permute-start.2 = (bf16[8,2,128,128]{3,2,1,0:T(8,128)(2,1)S(1)}, bf16[8,2,128,128]{3,2,1,0:T(8,128)(2,1)}, u32[]{:S(2)}, u32[]{:S(2)}) collective-permute-start(bf16[8,2,128,128]{3,2,1,0:T(8,128)(2,1)S(1)} %pad_maximum_fusion), channel_id=1, source_target_pairs={{0,2},{1,3},{2,4},{3,5},{4,6},{5,7},{6,8},{7,9},{8,10},{9,11},{10,... | collective-permute-start | bytes 1572872 | tf_op jit(solution)/shard_map/ppermute | solution.py:126
  60.8 58.4 %collective-permute-start.3 = (bf16[8,2,128,128]{3,2,1,0:T(8,128)(2,1)S(1)}, bf16[8,2,128,128]{3,2,1,0:T(8,128)(2,1)}, u32[]{:S(2)}, u32[]{:S(2)}) collective-permute-start(bf16[8,2,128,128]{3,2,1,0:T(8,128)(2,1)S(1)} %pad_maximum_fusion), channel_id=1, source_target_pairs={{0,1},{1,2},{2,3},{3,4},{4,5},{5,6},{6,7},{7,8},{8,9},{9,10},{10,1... | collective-permute-start | bytes 1572872 | tf_op jit(solution)/shard_map/ppermute | solution.py:126
  120.5 63.8 %copy-start = (bf16[36,2,128,128]{3,2,1,0:T(8,128)(2,1)}, bf16[36,2,128,128]{3,2,1,0:T(8,128)(2,1)S(1)}, u32[]{:S(2)}) copy-start(bf16[36,2,128,128]{3,2,1,0:T(8,128)(2,1)S(1)} %constant_dynamic-update-slice_fusion.ext_hbm) | copy-start | bytes 7077892
Sparse Core Ops, SparseCore 0:
  18.8 31.8 all-gather.4
  52.4 121.4 all-gather.6

commit v2 on v1

v2 whole, which is shorter than its diff:
```python
import functools, math
import jax, jax.numpy as jnp
from jax import lax
from jax.experimental import pallas as pl
from jax.experimental.pallas import tpu as pltpu
from jax.sharding import PartitionSpec as P

BLK = 128
NEG = -1e30
BACK = 28
F32 = jnp.float32
BF16 = jnp.bfloat16
SCALE2 = math.log2(math.e) / math.sqrt(128.0)


def dot(a, b):
    return jnp.dot(a, b, preferred_element_type=F32)


def lane_max(parts):
    top = parts[0]
    for part in parts[1:]:
        top = jnp.maximum(top, part)
    return jnp.max(top, axis=1, keepdims=True)


def lane_sum(parts):
    total = parts[0]
    for part in parts[1:]:
        total = total + part
    return jnp.sum(total, axis=1, keepdims=True)


def near_step(h, i, slab, slash_ref, q_ref, ext_ref, acc_ref, top_ref, sum_ref):
    rows = pl.ds(pl.multiple_of(i * BLK, BLK), BLK)
    q = q_ref[h, rows, :]
    row = lax.broadcasted_iota(jnp.int32, (BLK, BLK), 0)
    col = lax.broadcasted_iota(jnp.int32, (BLK, BLK), 1)
    own = BACK + i
    scores = [jnp.where(row >= col, dot(q, ext_ref[own, 0]), NEG)]
    blocks = [own]
    for n in range(0, 8, 2):
        pair, bias = [], []
        for k in (n, n + 1):
            off = slash_ref[h, k]
            ok = slab * 8 + i - off >= 0
            pair.append(jnp.where(ok, own - off, own))
            bias.append(jnp.where(ok, 0.0, NEG).astype(F32))
        both = dot(q, jnp.concatenate([ext_ref[pair[0], 0], ext_ref[pair[1], 0]], axis=1))
        scores.append(both[:, :BLK] + bias[0])
        scores.append(both[:, BLK:] + bias[1])
        blocks += pair
    top = lane_max(scores)
    weights = [jnp.exp2((s - top) * SCALE2) for s in scores]
    acc = dot(weights[0].astype(BF16), ext_ref[blocks[0], 1])
    for n in range(1, 9, 2):
        p = jnp.concatenate([weights[n].astype(BF16), weights[n + 1].astype(BF16)], axis=1)
        v = jnp.concatenate([ext_ref[blocks[n], 1], ext_ref[blocks[n + 1], 1]], axis=0)
        acc = acc + dot(p, v)
    acc_ref[h, rows, :] = acc
    top_ref[h, rows, :] = top
    sum_ref[h, rows, :] = lane_sum(weights)


def far_step(h, i, slab, slash_ref, vert_ref, pos_ref, q_ref, far_ref, acc_ref, top_ref, sum_ref, out_ref):
    rows = pl.ds(pl.multiple_of(i * BLK, BLK), BLK)
    q = q_ref[h, rows, :]
    mine = slab * 8 + i
    bias, places = [], []
    for k in range(8):
        name = vert_ref[h, k]
        gap = mine - name
        ok = gap > 0
        for n in range(8):
            ok = ok & (slash_ref[h, n] != gap)
        bias.append(jnp.where(ok, 0.0, NEG).astype(F32))
        places.append((pos_ref[h, k], pos_ref[8 + h, k]))
    scores = []
    for k in range(0, 8, 2):
        both = dot(q, jnp.concatenate([far_ref[places[k][0], places[k][1]], far_ref[places[k + 1][0], places[k + 1][1]]], axis=1))
        scores.append(both[:, :BLK] + bias[k])
        scores.append(both[:, BLK:] + bias[k + 1])
    old = top_ref[h, rows, :]
    top = jnp.maximum(old, lane_max(scores))
    keep = jnp.exp2((old - top) * SCALE2)
    weights = [jnp.exp2((s - top) * SCALE2) for s in scores]
    acc = None
    for k in range(0, 8, 2):
        p = jnp.concatenate([weights[k].astype(BF16), weights[k + 1].astype(BF16)], axis=1)
        v = jnp.concatenate([far_ref[places[k][0], places[k][1] + 1], far_ref[places[k + 1][0], places[k + 1][1] + 1]], axis=0)
        acc = dot(p, v) if acc is None else acc + dot(p, v)
    total = sum_ref[h, rows, :] * keep + lane_sum(weights)
    out_ref[h, rows, :] = ((acc_ref[h, rows, :] * keep + acc) / total).astype(BF16)


MESH = pl.DeviceIdType.MESH
UNROLL = 4
DIRS = (1, -1)
NAMES = ["y", "zP-", "zP+", "zP2", "hA", "hB", "h3", "h4", "y1", "y2", "y3"]
NAMES += [kind + str(d) for kind in ("xo", "xp", "x1", "x2", "x3", "ro", "r1", "r2", "r3") for d in DIRS]
NAMES += ["R" + str(j) + str(d) for j in (0, 1, -1, 2) for d in DIRS]
NAMES += ["RR" + str(j) for j in (0, 1, -1, 2)]
INDEX = {name: n for n, name in enumerate(NAMES)}


def kernel(slash, vert, place, which, q_hbm, k_hbm, v_hbm, out_hbm,
           q, raw, own, ext, far, acc, top, tot, out, load_sem, send_sem, recv_sem, part_sem, part_recv, keep_sem):
    group = lax.axis_index("head")
    slab = lax.axis_index("seq")
    x, z, half = slab // 8, (slab // 2) % 4, slab % 2
    loads = [
        pltpu.make_async_copy(k_hbm, raw, load_sem.at[8]),
        pltpu.make_async_copy(v_hbm, own.at[:, 1], load_sem.at[9]),
        pltpu.make_async_copy(v_hbm, ext.at[pl.ds(BACK, 8), 1], load_sem.at[10]),
    ]
    heads = [
        pltpu.make_async_copy(q_hbm.at[:, pl.ds(h * BLK, BLK)], q.at[h], load_sem.at[h]) for h in range(8)
    ]
    for load in loads + heads:
        load.start()

    def seat(dx, dz, dy):
        return ((x + dx) % 4) * 8 + ((z + dz) % 4) * 2 + ((half + dy) % 2)

    def spot(g, s):
        return (g, s)

    mate = spot(group, seat(0, 0, 1))
    after = spot(group, (slab + 2) % 32)
    before = spot(group, (slab + 30) % 32)
    across = {d: spot(group, seat(d, 0, 0)) for d in DIRS}
    along = {d: spot(group, seat(0, d, 0)) for d in DIRS}
    peers = [spot((group + n) % 4, slab) for n in (1, 2, 3)]
    barrier = pltpu.get_barrier_semaphore()
    friends = [mate, after, before, across[1], across[-1], along[1], along[-1]] + peers
    for friend in friends:
        pl.semaphore_signal(barrier, inc=1, device_id=friend, device_id_type=MESH)

    for load in loads:
        load.wait()
    for b in range(8):
        flipped = raw[b].astype(F32).T.astype(BF16)
        own[b, 0] = flipped
        ext[BACK + b, 0] = flipped
    for c in range(4):
        far[slab, 2 * c] = own[which[0, c], 0]
        far[slab, 2 * c + 1] = own[which[0, c], 1]
    pl.semaphore_wait(barrier, len(friends))

    PP, RR, ALL = (0, 5), (5, 3), (0, 8)

    def one(dx, dz, side, sub):
        return far.at[pl.ds(((x + dx) % 4) * 8 + ((z + dz) % 4) * 2 + side, 1), pl.ds(*sub)]

    def pair(dx, dz, sub):
        return far.at[pl.ds(((x + dx) % 4) * 8 + ((z + dz) % 4) * 2, 2), pl.ds(*sub)]

    def near(at, side_step=0):
        return ext.at[pl.ds(at + side_step * half, 4)]

    plan = {
        "y": (one(0, 0, half, ALL), None, mate, one(0, 0, 1 - half, ALL)),
        "zP-": (pair(0, 0, PP), None, along[-1], pair(0, 1, PP)),
        "zP+": (pair(0, 0, PP), None, along[1], pair(0, -1, PP)),
        "zP2": (pair(0, 1, PP), None, along[-1], pair(0, 2, PP)),
        "hA": (near(28), near(12), after, near(12)),
        "hB": (near(32), near(16), after, near(16)),
        "h4": (near(16), near(0), after, near(0)),
        "h3": (near(20), near(4), after, near(4)),
        "y1": (near(28, -16), near(20), mate, near(20)),
        "y2": (near(32, -16), near(24), mate, near(24)),
        "y3": (near(16, -16), near(8), mate, near(8)),
    }
    for d in DIRS:
        side = 0 if d == 1 else 1
        plan["xo" + str(d)] = (one(0, 0, half, ALL), None, across[d], one(-d, 0, half, ALL))
        plan["xp" + str(d)] = (one(0, 0, 1 - half, ALL), None, across[d], one(-d, 0, 1 - half, ALL))
        plan["ro" + str(d)] = (one(-d, 0, side, ALL), None, across[d], one(2, 0, side, ALL))
        for n, dz in (("1", 1), ("2", 2), ("3", -1)):
            plan["x" + n + str(d)] = (pair(0, dz, PP), None, across[d], pair(-d, dz, PP))
            plan["r" + n + str(d)] = (one(-d, dz, side, PP), None, across[d], one(2, dz, side, PP))
        for j in (0, 1, -1, 2):
            plan["R" + str(j) + str(d)] = (pair(j, 0, RR), None, along[d], pair(j, -d, RR))
    for j in (0, 1, -1, 2):
        d = 1 if j == 2 else -1
        plan["RR" + str(j)] = (pair(j, -d, RR), None, along[d], pair(j, 2, RR))

    def copy(name, landing):
        source, target, device, lands = plan[name]
        n = INDEX[name]
        return pltpu.make_async_remote_copy(
            src_ref=lands if landing else source,
            dst_ref=lands if landing else (source if target is None else target),
            send_sem=send_sem.at[n],
            recv_sem=recv_sem.at[n],
            device_id=device,
            device_id_type=MESH,
        )

    def send(*names):
        for name in names:
            copy(name, False).start()

    waited = []

    def take(*names):
        for name in names:
            copy(name, True).wait_recv()
            waited.append(name)

    send("y", "xo1", "xo-1", "hA", "hB")
    take("hA")
    send("y1")
    take("y")
    send("xp1", "xp-1", "zP-")
    take("hB")
    send("y2", "h4")
    take("y1")
    send("h3", "zP+")
    take("xo1", "xo-1", "xp1", "xp-1")
    send("ro1", "ro-1")
    take("zP-")
    send("zP2", "x11", "x1-1", "R01", "R0-1", "R11", "R1-1", "R-11", "R-1-1")
    take("h4")
    send("y3")
    take("ro1", "ro-1")
    send("R21", "R2-1")
    take("zP2")
    send("x21", "x2-1")
    for head in heads:
        head.wait()
    take("y2", "h3", "y3")

    def at_1():
        take("x11", "x1-1")
        send("r11", "r1-1")

    def at_3():
        take("zP+")
        send("x31", "x3-1")

    def at_6():
        take("R0-1", "R1-1", "R-1-1")
        send("RR0", "RR1", "RR-1")

    def at_8():
        take("x21", "x2-1")
        send("r21", "r2-1")

    def at_10():
        take("R21")
        send("RR2")

    def at_13():
        take("x31", "x3-1")
        send("r31", "r3-1")

    events = {1: at_1, 3: at_3, 6: at_6, 8: at_8, 10: at_10, 13: at_13}

    @pl.loop(0, 64 // UNROLL)
    def _(t):
        for when, event in events.items():
            pl.when(t == when)(event)
        for u in range(UNROLL):
            e = t * UNROLL + u
            near_step(e // 8, e % 8, slab, slash, q, ext, acc, top, tot)

    take(*[name for name in NAMES if name not in waited])

    def quarter(h, n):
        return out.at[h, pl.ds(((group + n) % 4) * 256, 256)]

    def column(h):
        return out_hbm.at[:, pl.ds(pl.multiple_of((group * 8 + h) * BLK, BLK), BLK)]

    def share(h, n):
        return pltpu.make_async_remote_copy(
            src_ref=quarter(h, n),
            dst_ref=column(h),
            send_sem=part_sem.at[h, n - 1],
            recv_sem=part_recv.at[h, n - 1],
            device_id=peers[n - 1],
            device_id_type=MESH,
        )

    def keep(h):
        return pltpu.make_async_copy(quarter(h, 0), column(h), keep_sem.at[h])

    @pl.loop(0, 8)
    def _(h):
        @pl.loop(0, 8 // UNROLL)
        def _(t):
            for u in range(UNROLL):
                far_step(h, t * UNROLL + u, slab, slash, vert, place, q, far, acc, top, tot, out)

        for n in (2, 1, 3):
            share(h, n).start()
        keep(h).start()

    for name in NAMES:
        copy(name, False).wait_send()

    @pl.loop(0, 8)
    def _(h):
        keep(h).wait()
        for n in (1, 2, 3):
            origin = (group - n + 4) % 4
            share(h, n).wait_send()
            lands = out_hbm.at[:, pl.ds(pl.multiple_of((origin * 8 + h) * BLK, BLK), BLK)]
            pltpu.make_async_remote_copy(
                src_ref=quarter(h, n),
                dst_ref=lands,
                send_sem=part_sem.at[h, n - 1],
                recv_sem=part_recv.at[h, n - 1],
                device_id=peers[n - 1],
                device_id_type=MESH,
            ).wait_recv()


def attention(slash, vert, place, which, q, k, v):
    whole = pl.BlockSpec(memory_space=pl.ANY)
    scalars = pl.BlockSpec(memory_space=pltpu.SMEM)
    return pl.pallas_call(
        kernel,
        out_shape=jax.ShapeDtypeStruct((256, 4096), BF16),
        in_specs=[scalars] * 4 + [whole] * 3,
        out_specs=whole,
        scratch_shapes=[
            pltpu.VMEM((8, 1024, 128), BF16),
            pltpu.VMEM((8, 128, 128), BF16),
            pltpu.VMEM((8, 2, 128, 128), BF16),
            pltpu.VMEM((36, 2, 128, 128), BF16),
            pltpu.VMEM((32, 8, 128, 128), BF16),
            pltpu.VMEM((8, 1024, 128), F32),
            pltpu.VMEM((8, 1024, 1), F32),
            pltpu.VMEM((8, 1024, 1), F32),
            pltpu.VMEM((8, 1024, 128), BF16),
            pltpu.SemaphoreType.DMA((11,)),
            pltpu.SemaphoreType.DMA((len(NAMES),)),
            pltpu.SemaphoreType.DMA((len(NAMES),)),
            pltpu.SemaphoreType.DMA((8, 3)),
            pltpu.SemaphoreType.DMA((8, 3)),
            pltpu.SemaphoreType.DMA((8,)),
        ],
        compiler_params=pltpu.CompilerParams(
            collective_id=0, has_side_effects=True, vmem_limit_bytes=60 * 2**20
        ),
    )(slash, vert, place, which, q, k, v)


def shards(queries, keys, values, vertical, slash):
    slab = lax.axis_index("seq")
    ids = jnp.arange(256, dtype=jnp.int32)
    flat = vertical.reshape(-1)
    used = jnp.any(flat[:, None] == ids[None, :], axis=0)
    earlier = used[None, :] & (ids[None, :] // 8 == flat[:, None] // 8) & (ids[None, :] < flat[:, None])
    rank = jnp.sum(earlier.astype(jnp.int32), axis=1)
    place = jnp.concatenate([vertical // 8, 2 * rank.reshape(8, 8)], axis=0)
    mine = flat[:, None] - slab * 8
    slots = jnp.arange(4, dtype=jnp.int32)[None, :]
    hit = (mine >= 0) & (mine < 8) & (rank[:, None] == slots)
    which = jnp.max(jnp.where(hit, mine, 0), axis=0, keepdims=True)
    return attention(
        slash, vertical, place, which, queries, keys.reshape(8, BLK, BLK), values.reshape(8, BLK, BLK)
    )


def solution(mesh):
    return jax.shard_map(
        shards,
        mesh=mesh,
        in_specs=(P("seq", "head"), P("seq", "head"), P("seq", "head"), P("head", None), P("head", None)),
        out_specs=P(("seq", "head"), None),
        check_vma=False,
    )
```

time: 285 us -> 123 us (0.43)
  the two profiles are of different devices: /device:TPU:7 before, /device:TPU:97 now
where the time goes in v2:
time: 123 us
  Pallas kernels  116 us (94%)
  local copies, waits for them, and re-layouts  3.97 us (3%)
  other arithmetic  2.25 us (2%)
    pallas_call x1, Pallas kernels, attention(): pl.pallas_call(kernel, out_shape=jax.ShapeDtypeStruct((256, 4096), BF16),...  116 us
    unnamed x1, local copies, waits for them, and re-layouts  3.13 us

profile of v2, /device:TPU:97, one launch (start us, length us, event | category | flops | bytes accessed | tf_op | source)
XLA Modules:
  0.0 122.5 jit_solution(17406452863158905826)
XLA Ops:
  0.0 0.8 eq.43
  0.8 0.1 fusion
  0.9 0.2 convert_reduce_fusion
  1.1 0.6 select_reduce_fusion
  1.7 0.1 mul.14
  1.8 0.7 add_select_fusion
  2.5 0.6 pad_add_fusion.place
  3.1 116.3 %shard_map.55 = bf16[256,4096]{1,0:T(8,128)(2,1)} custom-call(s32[8,8]{1,0:T(8,128)} %slash.1, s32[8,8]{1,0:T(8,128)} %vert.1, s32[16,8]{1,0:T(8,128)} %pad_add_fusion.place, s32[1,4]{1,0:T(1,128)} %bitcast.5, bf16[1024,1024]{1,0:T(8,128)(2,1)} %q_hbm.1, bf16[8,128,128]{2,1,0:T(8,128)(2,1)} %bitcast.3, bf16[8,128,128]{2,1,0:T(8,128)(2,1)} %bitcast.4), custom_call_target="tpu_custom_call" | custom-call | tf_op jit(solution)/shard_map/pallas_call | solution.py:323
  119.4 3.1 %copy.7 = bf16[256,4096]{1,0:T(8,128)(2,1)} copy(bf16[256,4096]{1,0:T(8,128)(2,1)} %shard_map.55) | data formatting | bytes 4194304
  (4 shorter events, 0.0 us)

commit v3 on v2

--- a/solution.py
+++ b/solution.py
@@ -31,80 +31,105 @@
     return jnp.sum(total, axis=1, keepdims=True)
 
 
-def near_step(h, i, slab, slash_ref, q_ref, ext_ref, acc_ref, top_ref, sum_ref):
+def cat_dot(ps, vs):
+    return dot(jnp.concatenate([p.astype(BF16) for p in ps], axis=1), jnp.concatenate(vs, axis=0))
+
+def near_scores(h, i, slab, slash_ref, q_ref, ext_ref):
     rows = pl.ds(pl.multiple_of(i * BLK, BLK), BLK)
     q = q_ref[h, rows, :]
     row = lax.broadcasted_iota(jnp.int32, (BLK, BLK), 0)
     col = lax.broadcasted_iota(jnp.int32, (BLK, BLK), 1)
     own = BACK + i
+    blocks = [own]
+    bias = []
+    for k in range(8):
+        off = slash_ref[h, k]
+        ok = slab * 8 + i - off >= 0
+        blocks.append(jnp.where(ok, own - off, own))
+        bias.append(jnp.where(ok, 0.0, NEG).astype(F32))
     scores = [jnp.where(row >= col, dot(q, ext_ref[own, 0]), NEG)]
-    blocks = [own]
-    for n in range(0, 8, 2):
-        pair, bias = [], []
-        for k in (n, n + 1):
-            off = slash_ref[h, k]
-            ok = slab * 8 + i - off >= 0
-            pair.append(jnp.where(ok, own - off, own))
-            bias.append(jnp.where(ok, 0.0, NEG).astype(F32))
-        both = dot(q, jnp.concatenate([ext_ref[pair[0], 0], ext_ref[pair[1], 0]], axis=1))
-        scores.append(both[:, :BLK] + bias[0])
-        scores.append(both[:, BLK:] + bias[1])
-        blocks += pair
-    top = lane_max(scores)
-    weights = [jnp.exp2((s - top) * SCALE2) for s in scores]
-    acc = dot(weights[0].astype(BF16), ext_ref[blocks[0], 1])
-    for n in range(1, 9, 2):
-        p = jnp.concatenate([weights[n].astype(BF16), weights[n + 1].astype(BF16)], axis=1)
-        v = jnp.concatenate([ext_ref[blocks[n], 1], ext_ref[blocks[n + 1], 1]], axis=0)
-        acc = acc + dot(p, v)
-    acc_ref[h, rows, :] = acc
-    top_ref[h, rows, :] = top
-    sum_ref[h, rows, :] = lane_sum(weights)
-
-
-def far_step(h, i, slab, slash_ref, vert_ref, pos_ref, q_ref, far_ref, acc_ref, top_ref, sum_ref, out_ref):
+    for k in range(0, 8, 2):
+        both = dot(q, jnp.concatenate([ext_ref[blocks[1 + k], 0], ext_ref[blocks[2 + k], 0]], axis=1))
+        scores.append(both[:, :BLK] + bias[k])
+        scores.append(both[:, BLK:] + bias[k + 1])
+    return scores, blocks, rows
+
+def far_scores(h, i, slab, slash_ref, vert_ref, pos_ref, q_ref, far_ref):
     rows = pl.ds(pl.multiple_of(i * BLK, BLK), BLK)
     q = q_ref[h, rows, :]
     mine = slab * 8 + i
     bias, places = [], []
     for k in range(8):
-        name = vert_ref[h, k]
-        gap = mine - name
+        gap = mine - vert_ref[h, k]
         ok = gap > 0
         for n in range(8):
             ok = ok & (slash_ref[h, n] != gap)
         bias.append(jnp.where(ok, 0.0, NEG).astype(F32))
-        places.append((pos_ref[h, k], pos_ref[8 + h, k]))
+        places.append((jnp.where(ok, pos_ref[h, k], slab), jnp.where(ok, pos_ref[8 + h, k], 0)))
     scores = []
     for k in range(0, 8, 2):
         both = dot(q, jnp.concatenate([far_ref[places[k][0], places[k][1]], far_ref[places[k + 1][0], places[k + 1][1]]], axis=1))
         scores.append(both[:, :BLK] + bias[k])
         scores.append(both[:, BLK:] + bias[k + 1])
-    old = top_ref[h, rows, :]
-    top = jnp.maximum(old, lane_max(scores))
-    keep = jnp.exp2((old - top) * SCALE2)
-    weights = [jnp.exp2((s - top) * SCALE2) for s in scores]
-    acc = None
-    for k in range(0, 8, 2):
-        p = jnp.concatenate([weights[k].astype(BF16), weights[k + 1].astype(BF16)], axis=1)
-        v = jnp.concatenate([far_ref[places[k][0], places[k][1] + 1], far_ref[places[k + 1][0], places[k + 1][1] + 1]], axis=0)
-        acc = dot(p, v) if acc is None else acc + dot(p, v)
-    total = sum_ref[h, rows, :] * keep + lane_sum(weights)
-    out_ref[h, rows, :] = ((acc_ref[h, rows, :] * keep + acc) / total).astype(BF16)
+    return scores, places, rows
+
+def near_put(slot, e, slab, slash, q, ext, stage):
+    scores, _, _ = near_scores(e // 8, e % 8, slab, slash, q, ext)
+    for k, s in enumerate(scores):
+        stage[slot, k] = s
+
+
+def near_finish(slot, e, slab, slash, ext, acc, top, tot, stage):
+    h, i = e // 8, e % 8
+    rows = pl.ds(pl.multiple_of(i * BLK, BLK), BLK)
+    own = BACK + i
+    blocks = [own]
+    for k in range(8):
+        off = slash[h, k]
+        blocks.append(jnp.where(slab * 8 + i - off >= 0, own - off, own))
+    scores = [stage[slot, k] for k in range(9)]
+    best = lane_max(scores)
+    weights = [jnp.exp2((s - best) * SCALE2) for s in scores]
+    acc[h, rows, :] = cat_dot(weights, [ext[b, 1] for b in blocks])
+    top[h, rows, :] = best
+    tot[h, rows, :] = lane_sum(weights)
+
+
+def far_put(slot, e, slab, slash, vert, pos, q, far, stage, spots):
+    scores, places, _ = far_scores(e // 8, e % 8, slab, slash, vert, pos, q, far)
+    for k, s in enumerate(scores):
+        stage[slot, k] = s
+        spots[slot, k] = places[k][0]
+        spots[slot, 8 + k] = places[k][1]
+
+
+def far_finish(slot, e, far, acc, top, tot, out, stage, spots):
+    h, i = e // 8, e % 8
+    rows = pl.ds(pl.multiple_of(i * BLK, BLK), BLK)
+    scores = [stage[slot, k] for k in range(8)]
+    old = top[h, rows, :]
+    best = jnp.maximum(old, lane_max(scores))
+    keep = jnp.exp2((old - best) * SCALE2)
+    weights = [jnp.exp2((s - best) * SCALE2) for s in scores]
+    mixed = cat_dot(weights, [far[spots[slot, k], spots[slot, 8 + k] + 1] for k in range(8)])
+    total = tot[h, rows, :] * keep + lane_sum(weights)
+    out[h, rows, :] = ((acc[h, rows, :] * keep + mixed) / total).astype(BF16)
 
 
 MESH = pl.DeviceIdType.MESH
-UNROLL = 4
+NEAR_STEPS = 4
+FAR_STEPS = 4
 DIRS = (1, -1)
 NAMES = ["y", "zP-", "zP+", "zP2", "hA", "hB", "h3", "h4", "y1", "y2", "y3"]
-NAMES += [kind + str(d) for kind in ("xo", "xp", "x1", "x2", "x3", "ro", "r1", "r2", "r3") for d in DIRS]
-NAMES += ["R" + str(j) + str(d) for j in (0, 1, -1, 2) for d in DIRS]
-NAMES += ["RR" + str(j) for j in (0, 1, -1, 2)]
+NAMES += [kind + str(d) for kind in ("xo", "xp", "x1", "x2", "x3") for d in DIRS]
+NAMES += ["ro", "rp", "r1", "r2", "r3"]
+NAMES += ["R" + str(j) + str(d) for j in (0, 1, 2, 3) for d in DIRS]
+NAMES += ["RR" + str(j) for j in (0, 1, 2, 3)]
 INDEX = {name: n for n, name in enumerate(NAMES)}
 
 
 def kernel(slash, vert, place, which, q_hbm, k_hbm, v_hbm, out_hbm,
-           q, raw, own, ext, far, acc, top, tot, out, load_sem, send_sem, recv_sem, part_sem, part_recv, keep_sem):
+           q, raw, own, ext, far, acc, top, tot, out, stage, spots, load_sem, send_sem, recv_sem, part_sem, part_recv, keep_sem):
     group = lax.axis_index("head")
     slab = lax.axis_index("seq")
     x, z, half = slab // 8, (slab // 2) % 4, slab % 2
@@ -147,7 +172,7 @@
         far[slab, 2 * c + 1] = own[which[0, c], 1]
     pl.semaphore_wait(barrier, len(friends))
 
-    PP, RR, ALL = (0, 5), (5, 3), (0, 8)
+    PP, RR, ALL = (0, 4), (4, 4), (0, 8)
 
     def one(dx, dz, side, sub):
         return far.at[pl.ds(((x + dx) % 4) * 8 + ((z + dz) % 4) * 2 + side, 1), pl.ds(*sub)]
@@ -171,19 +196,39 @@
         "y2": (near(32, -16), near(24), mate, near(24)),
         "y3": (near(16, -16), near(8), mate, near(8)),
     }
+    sends = {d: x < 3 if d == 1 else x < 2 for d in DIRS}
+    takes = {d: x > 0 if d == 1 else (x == 3) | (x == 0) for d in DIRS}
+    sender, taker = {}, {}
     for d in DIRS:
-        side = 0 if d == 1 else 1
-        plan["xo" + str(d)] = (one(0, 0, half, ALL), None, across[d], one(-d, 0, half, ALL))
-        plan["xp" + str(d)] = (one(0, 0, 1 - half, ALL), None, across[d], one(-d, 0, 1 - half, ALL))
-        plan["ro" + str(d)] = (one(-d, 0, side, ALL), None, across[d], one(2, 0, side, ALL))
-        for n, dz in (("1", 1), ("2", 2), ("3", -1)):
-            plan["x" + n + str(d)] = (pair(0, dz, PP), None, across[d], pair(-d, dz, PP))
-            plan["r" + n + str(d)] = (one(-d, dz, side, PP), None, across[d], one(2, dz, side, PP))
-        for j in (0, 1, -1, 2):
-            plan["R" + str(j) + str(d)] = (pair(j, 0, RR), None, along[d], pair(j, -d, RR))
-    for j in (0, 1, -1, 2):
+        for n, source, lands in (
+            ("xo", one(0, 0, half, ALL), one(-d, 0, half, ALL)),
+            ("xp", one(0, 0, 1 - half, ALL), one(-d, 0, 1 - half, ALL)),
+            ("x1", pair(0, 1, PP), pair(-d, 1, PP)),
+            ("x2", pair(0, 2, PP), pair(-d, 2, PP)),
+            ("x3", pair(0, -1, PP), pair(-d, -1, PP)),
+        ):
+            plan[n + str(d)] = (source, None, across[d], lands)
+            sender[n + str(d)] = sends[d]
+            taker[n + str(d)] = takes[d]
+        for j in (0, 1, 2, 3):
+            plan["R" + str(j) + str(d)] = (pair(-j, 0, RR), None, along[d], pair(-j, -d, RR))
+            if j:
+                sender["R" + str(j) + str(d)] = taker["R" + str(j) + str(d)] = x >= j
+    for n, source, lands in (
+        ("ro", one(1, 0, half, ALL), one(2, 0, half, ALL)),
+        ("rp", one(1, 0, 1 - half, ALL), one(2, 0, 1 - half, ALL)),
+        ("r1", pair(1, 1, PP), pair(2, 1, PP)),
+        ("r2", pair(1, 2, PP), pair(2, 2, PP)),
+        ("r3", pair(1, -1, PP), pair(2, -1, PP)),
+    ):
+        plan[n] = (source, None, across[-1], lands)
+        sender[n] = (x == 0) | (x == 3)
+        taker[n] = (x == 3) | (x == 2)
+    for j in (0, 1, 2, 3):
         d = 1 if j == 2 else -1
-        plan["RR" + str(j)] = (pair(j, -d, RR), None, along[d], pair(j, 2, RR))
+        plan["RR" + str(j)] = (pair(-j, -d, RR), None, along[d], pair(-j, 2, RR))
+        if j:
+            sender["RR" + str(j)] = taker["RR" + str(j)] = x >= j
 
     def copy(name, landing):
         source, target, device, lands = plan[name]
@@ -197,15 +242,21 @@
             device_id_type=MESH,
         )
 
+    def guarded(rule, name, act):
+        if name in rule:
+            pl.when(rule[name])(act)
+        else:
+            act()
+
     def send(*names):
         for name in names:
-            copy(name, False).start()
+            guarded(sender, name, lambda name=name: copy(name, False).start())
 
     waited = []
 
     def take(*names):
         for name in names:
-            copy(name, True).wait_recv()
+            guarded(taker, name, lambda name=name: copy(name, True).wait_recv())
             waited.append(name)
 
     send("y", "xo1", "xo-1", "hA", "hB")
@@ -218,13 +269,11 @@
     take("y1")
     send("h3", "zP+")
     take("xo1", "xo-1", "xp1", "xp-1")
-    send("ro1", "ro-1")
+    send("ro", "rp")
     take("zP-")
-    send("zP2", "x11", "x1-1", "R01", "R0-1", "R11", "R1-1", "R-11", "R-1-1")
+    send("zP2", "x11", "x1-1", "R11", "R1-1", "R01", "R0-1")
     take("h4")
     send("y3")
-    take("ro1", "ro-1")
-    send("R21", "R2-1")
     take("zP2")
     send("x21", "x2-1")
     for head in heads:
@@ -233,38 +282,47 @@
 
     def at_1():
         take("x11", "x1-1")
-        send("r11", "r1-1")
-
-    def at_3():
+        send("r1")
+
+    def at_2():
         take("zP+")
         send("x31", "x3-1")
 
-    def at_6():
-        take("R0-1", "R1-1", "R-1-1")
-        send("RR0", "RR1", "RR-1")
-
-    def at_8():
+    def at_3():
+        take("ro", "rp")
+        send("R31", "R3-1", "R21", "R2-1")
+
+    def at_5():
+        take("R0-1", "R1-1")
+        send("RR0", "RR1")
+
+    def at_7():
         take("x21", "x2-1")
-        send("r21", "r2-1")
-
-    def at_10():
-        take("R21")
-        send("RR2")
-
-    def at_13():
+        send("r2")
+
+    def at_9():
+        take("R3-1", "R21")
+        send("RR3", "RR2")
+
+    def at_12():
         take("x31", "x3-1")
-        send("r31", "r3-1")
-
-    events = {1: at_1, 3: at_3, 6: at_6, 8: at_8, 10: at_10, 13: at_13}
-
-    @pl.loop(0, 64 // UNROLL)
+        send("r3")
+
+    events = {2: at_1, 5: at_2, 7: at_3, 10: at_5}
+    near_put(0, 0, slab, slash, q, ext, stage)
+
+    @pl.loop(0, 64 // NEAR_STEPS)
     def _(t):
         for when, event in events.items():
             pl.when(t == when)(event)
-        for u in range(UNROLL):
-            e = t * UNROLL + u
-            near_step(e // 8, e % 8, slab, slash, q, ext, acc, top, tot)
-
+        for u in range(NEAR_STEPS):
+            e = t * NEAR_STEPS + u
+            near_put((u + 1) % 2, jnp.minimum(e + 1, 63), slab, slash, q, ext, stage)
+            near_finish(u % 2, e, slab, slash, ext, acc, top, tot, stage)
+
+    at_7()
+    at_9()
+    at_12()
     take(*[name for name in NAMES if name not in waited])
 
     def quarter(h, n):
@@ -286,19 +344,23 @@
     def keep(h):
         return pltpu.make_async_copy(quarter(h, 0), column(h), keep_sem.at[h])
 
+    far_put(0, 0, slab, slash, vert, place, q, far, stage, spots)
+
     @pl.loop(0, 8)
     def _(h):
-        @pl.loop(0, 8 // UNROLL)
+        @pl.loop(0, 8 // FAR_STEPS)
         def _(t):
-            for u in range(UNROLL):
-                far_step(h, t * UNROLL + u, slab, slash, vert, place, q, far, acc, top, tot, out)
+            for u in range(FAR_STEPS):
+                e = h * 8 + t * FAR_STEPS + u
+                far_put((u + 1) % 2, jnp.minimum(e + 1, 63), slab, slash, vert, place, q, far, stage, spots)
+                far_finish(u % 2, e, far, acc, top, tot, out, stage, spots)
 
         for n in (2, 1, 3):
             share(h, n).start()
         keep(h).start()
 
     for name in NAMES:
-        copy(name, False).wait_send()
+        guarded(sender, name, lambda name=name: copy(name, False).wait_send())
 
     @pl.loop(0, 8)
     def _(h):
@@ -335,6 +397,8 @@
             pltpu.VMEM((8, 1024, 1), F32),
             pltpu.VMEM((8, 1024, 1), F32),
             pltpu.VMEM((8, 1024, 128), BF16),
+            pltpu.VMEM((2, 9, 128, 128), F32),
+            pltpu.SMEM((2, 16), jnp.int32),
             pltpu.SemaphoreType.DMA((11,)),
             pltpu.SemaphoreType.DMA((len(NAMES),)),
             pltpu.SemaphoreType.DMA((len(NAMES),)),

time: 123 us -> 114 us (0.927)
  the two profiles are of different devices: /device:TPU:97 before, /device:TPU:71 now
where the time goes in v3:
time: 114 us
  Pallas kernels  108 us (95%)
  local copies, waits for them, and re-layouts  3.97 us (3%)
  other arithmetic  2.25 us (2%)
    pallas_call x1, Pallas kernels, attention(): pl.pallas_call(kernel, out_shape=jax.ShapeDtypeStruct((256, 4096), BF16),...  108 us
    unnamed x1, local copies, waits for them, and re-layouts  3.13 us

profile of v3, /device:TPU:71, one launch (start us, length us, event | category | flops | bytes accessed | tf_op | source)
XLA Modules:
  0.0 114.2 jit_solution(7390899093130570171)
XLA Ops:
  0.0 0.8 eq.43
  0.8 0.1 fusion
  0.9 0.2 convert_reduce_fusion
  1.1 0.6 select_reduce_fusion
  1.7 0.1 mul.14
  1.8 0.7 add_select_fusion
  2.5 0.6 pad_add_fusion.place
  3.1 108.0 %shard_map.55 = bf16[256,4096]{1,0:T(8,128)(2,1)} custom-call(s32[8,8]{1,0:T(8,128)} %slash.1, s32[8,8]{1,0:T(8,128)} %vert.1, s32[16,8]{1,0:T(8,128)} %pad_add_fusion.place, s32[1,4]{1,0:T(1,128)} %bitcast.5, bf16[1024,1024]{1,0:T(8,128)(2,1)} %q_hbm.1, bf16[8,128,128]{2,1,0:T(8,128)(2,1)} %bitcast.3, bf16[8,128,128]{2,1,0:T(8,128)(2,1)} %bitcast.4), custom_call_target="tpu_custom_call" | custom-call | tf_op jit(solution)/shard_map/pallas_call | solution.py:385
  111.1 3.1 %copy.7 = bf16[256,4096]{1,0:T(8,128)(2,1)} copy(bf16[256,4096]{1,0:T(8,128)(2,1)} %shard_map.55) | data formatting | bytes 4194304
  (4 shorter events, 0.0 us)

commit v4 on v3

--- a/solution.py
+++ b/solution.py
@@ -120,11 +120,39 @@
 NEAR_STEPS = 4
 FAR_STEPS = 4
 DIRS = (1, -1)
-NAMES = ["y", "zP-", "zP+", "zP2", "hA", "hB", "h3", "h4", "y1", "y2", "y3"]
+NAMES = ["y", "zP2", "hA", "hB", "h3", "h4", "y1", "y2", "y3", "ro", "rp"]
 NAMES += [kind + str(d) for kind in ("xo", "xp", "x1", "x2", "x3") for d in DIRS]
-NAMES += ["ro", "rp", "r1", "r2", "r3"]
-NAMES += ["R" + str(j) + str(d) for j in (0, 1, 2, 3) for d in DIRS]
+NAMES += [kind + n for kind in ("r", "s", "yr", "yq") for n in "123"]
+NAMES += ["R" + str(j) + str(d) for j in (1, 2, 3) for d in DIRS]
 NAMES += ["RR" + str(j) for j in (0, 1, 2, 3)]
+NAMES += [kind + str(d) + n for kind in ("zP", "R0") for d in DIRS for n in "op"]
+UPWARD = (2,)
+BEFORE = (
+    "+y", "+hA", "+hB", "+xo-1", "+zP-1o", "+R0-1o", "+xo1", "-y",
+    "+xp-1", "+zP-1p", "+zP1o", "+zP1p", "-hA", "+y1", "+R0-1p", "-xo-1",
+    "+ro", "-hB", "+h4", "-xp-1", "+rp", "-zP-1o", "-zP-1p", "+zP2",
+    "-y1", "+h3", "+y2", "+x1-1", "-xo1", "+R11", "+x11", "+R3-1",
+    "-zP2", "+x2-1", "+x21", "+R01p", "-h4", "+y3", "-zP1o", "-zP1p",
+    "+x3-1", "-ro", "-rp", "+R21", "+R1-1", "-R1-1", "+RR1", "+yq1",
+    "+x31", "-R0-1o", "-R0-1p", "+RR0", "-x1-1", "+r1", "-h3", "-y2",
+    "-y3",
+)
+DURING = {
+    1: ("-x2-1", "+r2",),
+    2: ("+R01o",),
+    3: ("+s2", "-RR1", "+yq2", "+xp1", "-R11", "+yq3",),
+    6: ("+R31", "-R3-1", "+RR3",),
+    7: ("+R2-1", "-x3-1", "+r3",),
+    8: ("-R21", "+RR2", "+s1",),
+    9: ("-r1", "+yr1",),
+    11: ("-r2", "+yr2", "+s3",),
+    12: ("-r3", "+yr3",),
+}
+AFTER = (
+    "-R01o", "-R01p", "-xp1", "-x11", "-x21", "-x31", "-R31", "-R2-1",
+    "-s1", "-yr1", "-yq1", "-s2", "-yr2", "-yq2", "-s3", "-yr3",
+    "-yq3", "-RR0", "-RR2", "-RR3",
+)
 INDEX = {name: n for n, name in enumerate(NAMES)}
 
 
@@ -185,8 +213,6 @@
 
     plan = {
         "y": (one(0, 0, half, ALL), None, mate, one(0, 0, 1 - half, ALL)),
-        "zP-": (pair(0, 0, PP), None, along[-1], pair(0, 1, PP)),
-        "zP+": (pair(0, 0, PP), None, along[1], pair(0, -1, PP)),
         "zP2": (pair(0, 1, PP), None, along[-1], pair(0, 2, PP)),
         "hA": (near(28), near(12), after, near(12)),
         "hB": (near(32), near(16), after, near(16)),
@@ -210,23 +236,35 @@
             plan[n + str(d)] = (source, None, across[d], lands)
             sender[n + str(d)] = sends[d]
             taker[n + str(d)] = takes[d]
-        for j in (0, 1, 2, 3):
-            plan["R" + str(j) + str(d)] = (pair(-j, 0, RR), None, along[d], pair(-j, -d, RR))
-            if j:
-                sender["R" + str(j) + str(d)] = taker["R" + str(j) + str(d)] = x >= j
+        for n, side in (("o", half), ("p", 1 - half)):
+            plan["zP" + str(d) + n] = (one(0, 0, side, PP), None, along[d], one(0, -d, side, PP))
+            plan["R0" + str(d) + n] = (one(0, 0, side, RR), None, along[d], one(0, -d, side, RR))
+        for j in (1, 2, 3):
+            part = (lambda dz: one(-1, dz, half, RR)) if j == 1 else (lambda dz, j=j: pair(-j, dz, RR))
+            plan["R" + str(j) + str(d)] = (part(0), None, along[d], part(-d))
+            sender["R" + str(j) + str(d)] = taker["R" + str(j) + str(d)] = x >= j
     for n, source, lands in (
         ("ro", one(1, 0, half, ALL), one(2, 0, half, ALL)),
         ("rp", one(1, 0, 1 - half, ALL), one(2, 0, 1 - half, ALL)),
-        ("r1", pair(1, 1, PP), pair(2, 1, PP)),
-        ("r2", pair(1, 2, PP), pair(2, 2, PP)),
-        ("r3", pair(1, -1, PP), pair(2, -1, PP)),
+        ("r1", one(1, 1, half, PP), one(2, 1, half, PP)),
+        ("r2", one(1, 2, half, PP), one(2, 2, half, PP)),
+        ("r3", one(1, -1, half, PP), one(2, -1, half, PP)),
     ):
         plan[n] = (source, None, across[-1], lands)
         sender[n] = (x == 0) | (x == 3)
         taker[n] = (x == 3) | (x == 2)
+    for n, dz in (("1", 1), ("2", 2), ("3", -1)):
+        plan["s" + n] = (one(1, dz, 1 - half, PP), None, across[-1], one(2, dz, 1 - half, PP))
+        sender["s" + n] = x == 3
+        taker["s" + n] = x == 2
+        plan["yr" + n] = (one(2, dz, half, PP), None, mate, one(2, dz, 1 - half, PP))
+        sender["yr" + n] = taker["yr" + n] = x == 3
+        plan["yq" + n] = (one(-1, dz, half, RR), None, mate, one(-1, dz, 1 - half, RR))
+        sender["yq" + n] = taker["yq" + n] = x >= 1
     for j in (0, 1, 2, 3):
-        d = 1 if j == 2 else -1
-        plan["RR" + str(j)] = (pair(-j, -d, RR), None, along[d], pair(-j, 2, RR))
+        d = 1 if j in UPWARD else -1
+        part = (lambda dz: one(-1, dz, half, RR)) if j == 1 else (lambda dz, j=j: pair(-j, dz, RR))
+        plan["RR" + str(j)] = (part(-d), None, along[d], part(2))
         if j:
             sender["RR" + str(j)] = taker["RR" + str(j)] = x >= j
 
@@ -259,70 +297,26 @@
             guarded(taker, name, lambda name=name: copy(name, True).wait_recv())
             waited.append(name)
 
-    send("y", "xo1", "xo-1", "hA", "hB")
-    take("hA")
-    send("y1")
-    take("y")
-    send("xp1", "xp-1", "zP-")
-    take("hB")
-    send("y2", "h4")
-    take("y1")
-    send("h3", "zP+")
-    take("xo1", "xo-1", "xp1", "xp-1")
-    send("ro", "rp")
-    take("zP-")
-    send("zP2", "x11", "x1-1", "R11", "R1-1", "R01", "R0-1")
-    take("h4")
-    send("y3")
-    take("zP2")
-    send("x21", "x2-1")
+    def run(steps):
+        for step in steps:
+            (take if step[0] == "-" else send)(step[1:])
+
+    run(BEFORE)
     for head in heads:
         head.wait()
-    take("y2", "h3", "y3")
-
-    def at_1():
-        take("x11", "x1-1")
-        send("r1")
-
-    def at_2():
-        take("zP+")
-        send("x31", "x3-1")
-
-    def at_3():
-        take("ro", "rp")
-        send("R31", "R3-1", "R21", "R2-1")
-
-    def at_5():
-        take("R0-1", "R1-1")
-        send("RR0", "RR1")
-
-    def at_7():
-        take("x21", "x2-1")
-        send("r2")
-
-    def at_9():
-        take("R3-1", "R21")
-        send("RR3", "RR2")
-
-    def at_12():
-        take("x31", "x3-1")
-        send("r3")
-
-    events = {2: at_1, 5: at_2, 7: at_3, 10: at_5}
+
     near_put(0, 0, slab, slash, q, ext, stage)
 
     @pl.loop(0, 64 // NEAR_STEPS)
     def _(t):
-        for when, event in events.items():
-            pl.when(t == when)(event)
+        for when, steps in DURING.items():
+            pl.when(t == when)(functools.partial(run, steps))
         for u in range(NEAR_STEPS):
             e = t * NEAR_STEPS + u
             near_put((u + 1) % 2, jnp.minimum(e + 1, 63), slab, slash, q, ext, stage)
             near_finish(u % 2, e, slab, slash, ext, acc, top, tot, stage)
 
-    at_7()
-    at_9()
-    at_12()
+    run(AFTER)
     take(*[name for name in NAMES if name not in waited])
 
     def quarter(h, n):

time: 114 us -> 98.1 us (0.86)
  the two profiles are of different devices: /device:TPU:71 before, /device:TPU:7 now
where the time goes in v4:
time: 98.1 us; the launch traced here: 97.8 us
  Pallas kernels  91.6 us (93%)
  local copies, waits for them, and re-layouts  3.97 us (4%)
  other arithmetic  2.25 us (2%)
    pallas_call x1, Pallas kernels, attention(): pl.pallas_call(kernel, out_shape=jax.ShapeDtypeStruct((256, 4096), BF16),...  91.6 us
    unnamed x1, local copies, waits for them, and re-layouts  3.13 us

profile of v4, /device:TPU:7, one launch (start us, length us, event | category | flops | bytes accessed | tf_op | source)
XLA Modules:
  0.0 97.8 jit_solution(17266464376791948897)
XLA Ops:
  0.0 0.8 eq.43
  0.8 0.1 fusion
  0.9 0.2 convert_reduce_fusion
  1.1 0.6 select_reduce_fusion
  1.7 0.1 mul.14
  1.8 0.7 add_select_fusion
  2.5 0.6 pad_add_fusion.place
  3.1 91.6 %shard_map.55 = bf16[256,4096]{1,0:T(8,128)(2,1)} custom-call(s32[8,8]{1,0:T(8,128)} %slash.1, s32[8,8]{1,0:T(8,128)} %vert.1, s32[16,8]{1,0:T(8,128)} %pad_add_fusion.place, s32[1,4]{1,0:T(1,128)} %bitcast.5, bf16[1024,1024]{1,0:T(8,128)(2,1)} %q_hbm.1, bf16[8,128,128]{2,1,0:T(8,128)(2,1)} %bitcast.3, bf16[8,128,128]{2,1,0:T(8,128)(2,1)} %bitcast.4), custom_call_target="tpu_custom_call" | custom-call | tf_op jit(solution)/shard_map/pallas_call | solution.py:379
  94.7 3.1 %copy.7 = bf16[256,4096]{1,0:T(8,128)(2,1)} copy(bf16[256,4096]{1,0:T(8,128)(2,1)} %shard_map.55) | data formatting | bytes 4194304
  (4 shorter events, 0.0 us)

commit v5 on v4

--- a/solution.py
+++ b/solution.py
@@ -348,10 +348,10 @@
                 e = h * 8 + t * FAR_STEPS + u
                 far_put((u + 1) % 2, jnp.minimum(e + 1, 63), slab, slash, vert, place, q, far, stage, spots)
                 far_finish(u % 2, e, far, acc, top, tot, out, stage, spots)
-
-        for n in (2, 1, 3):
-            share(h, n).start()
-        keep(h).start()
+            for n in (2, 1, 3):
+                pl.when(((group + n) % 4) // 2 == t)(lambda n=n: share(h, n).start())
+            pl.when(group // 2 == t)(lambda: keep(h).start())
+
 
     for name in NAMES:
         guarded(sender, name, lambda name=name: copy(name, False).wait_send())

time: 98.1 us -> 97.1 us (0.990)
  Pallas kernels: 91.6 us -> 90.3 us
    pallas_call x1, Pallas kernels: 91.6 us -> 90.3 us  [attention(): pl.pallas_call(kernel, out_shape=jax.ShapeDtypeStruct((256, 4096), BF16),...]
where the time goes in v5:
time: 97.1 us; the launch traced here: 96.6 us
  Pallas kernels  90.3 us (93%)
  local copies, waits for them, and re-layouts  3.97 us (4%)
  other arithmetic  2.25 us (2%)
    pallas_call x1, Pallas kernels, attention(): pl.pallas_call(kernel, out_shape=jax.ShapeDtypeStruct((256, 4096), BF16),...  90.3 us
    unnamed x1, local copies, waits for them, and re-layouts  3.13 us

profile of v5, /device:TPU:7, one launch (start us, length us, event | category | flops | bytes accessed | tf_op | source)
XLA Modules:
  0.0 96.6 jit_solution(7725205231651331175)
XLA Ops:
  0.0 0.8 eq.43
  0.8 0.1 fusion
  0.9 0.2 convert_reduce_fusion
  1.1 0.6 select_reduce_fusion
  1.7 0.1 mul.14
  1.8 0.7 add_select_fusion
  2.5 0.6 pad_add_fusion.place
  3.1 90.3 %shard_map.55 = bf16[256,4096]{1,0:T(8,128)(2,1)} custom-call(s32[8,8]{1,0:T(8,128)} %slash.1, s32[8,8]{1,0:T(8,128)} %vert.1, s32[16,8]{1,0:T(8,128)} %pad_add_fusion.place, s32[1,4]{1,0:T(1,128)} %bitcast.5, bf16[1024,1024]{1,0:T(8,128)(2,1)} %q_hbm.1, bf16[8,128,128]{2,1,0:T(8,128)(2,1)} %bitcast.3, bf16[8,128,128]{2,1,0:T(8,128)(2,1)} %bitcast.4), custom_call_target="tpu_custom_call" | custom-call | tf_op jit(solution)/shard_map/pallas_call | solution.py:379
  93.5 3.1 %copy.7 = bf16[256,4096]{1,0:T(8,128)(2,1)} copy(bf16[256,4096]{1,0:T(8,128)(2,1)} %shard_map.55) | data formatting | bytes 4194304
  (4 shorter events, 0.0 us)

commit v6 on v5

--- a/solution.py
+++ b/solution.py
@@ -156,8 +156,17 @@
 INDEX = {name: n for n, name in enumerate(NAMES)}
 
 
-def kernel(slash, vert, place, which, q_hbm, k_hbm, v_hbm, out_hbm,
-           q, raw, own, ext, far, acc, top, tot, out, stage, spots, load_sem, send_sem, recv_sem, part_sem, part_recv, keep_sem):
+def seen(vert, slab):
+    mask = jnp.int32(0)
+    for h in range(8):
+        for k in range(8):
+            name = vert[h, k]
+            mask = mask | jnp.where((name >> 3) == slab, jnp.int32(1) << (name & 7), 0)
+    return mask
+
+
+def kernel(slash, vert, q_hbm, k_hbm, v_hbm, out_hbm,
+           q, raw, own, ext, far, acc, top, tot, out, stage, spots, marks, place, load_sem, send_sem, recv_sem, part_sem, part_recv, keep_sem):
     group = lax.axis_index("head")
     slab = lax.axis_index("seq")
     x, z, half = slab // 8, (slab // 2) % 4, slab % 2
@@ -189,6 +198,13 @@
     for friend in friends:
         pl.semaphore_signal(barrier, inc=1, device_id=friend, device_id_type=MESH)
 
+    mask, count, chosen = seen(vert, slab), jnp.int32(0), [jnp.int32(0)] * 4
+    for b in range(8):
+        bit = (mask >> b) & 1
+        for c in range(4):
+            chosen[c] = jnp.where((bit == 1) & (count == c), b, chosen[c])
+        count = count + bit
+
     for load in loads:
         load.wait()
     for b in range(8):
@@ -196,8 +212,8 @@
         own[b, 0] = flipped
         ext[BACK + b, 0] = flipped
     for c in range(4):
-        far[slab, 2 * c] = own[which[0, c], 0]
-        far[slab, 2 * c + 1] = own[which[0, c], 1]
+        far[slab, 2 * c] = own[chosen[c], 0]
+        far[slab, 2 * c + 1] = own[chosen[c], 1]
     pl.semaphore_wait(barrier, len(friends))
 
     PP, RR, ALL = (0, 4), (4, 4), (0, 8)
@@ -301,7 +317,24 @@
         for step in steps:
             (take if step[0] == "-" else send)(step[1:])
 
-    run(BEFORE)
+    first = [step[0] for step in BEFORE].index("-")
+    run(BEFORE[:first])
+
+    @pl.loop(0, 32)
+    def _(s):
+        marks[s] = seen(vert, s)
+
+    @pl.loop(0, 8)
+    def _(h):
+        for k in range(8):
+            name = vert[h, k]
+            lower = marks[(name >> 3) & 31] & ((jnp.int32(1) << (name & 7)) - 1)
+            lower = lower - ((lower >> 1) & 0x55)
+            lower = (lower & 0x33) + ((lower >> 2) & 0x33)
+            place[h, k] = (name >> 3) & 31
+            place[8 + h, k] = 2 * ((lower + (lower >> 4)) & 3)
+
+    run(BEFORE[first:])
     for head in heads:
         head.wait()
 
@@ -373,13 +406,13 @@
             ).wait_recv()
 
 
-def attention(slash, vert, place, which, q, k, v):
+def attention(slash, vert, q, k, v):
     whole = pl.BlockSpec(memory_space=pl.ANY)
     scalars = pl.BlockSpec(memory_space=pltpu.SMEM)
     return pl.pallas_call(
         kernel,
         out_shape=jax.ShapeDtypeStruct((256, 4096), BF16),
-        in_specs=[scalars] * 4 + [whole] * 3,
+        in_specs=[scalars] * 2 + [whole] * 3,
         out_specs=whole,
         scratch_shapes=[
             pltpu.VMEM((8, 1024, 128), BF16),
@@ -393,6 +426,8 @@
             pltpu.VMEM((8, 1024, 128), BF16),
             pltpu.VMEM((2, 9, 128, 128), F32),
             pltpu.SMEM((2, 16), jnp.int32),
+            pltpu.SMEM((32,), jnp.int32),
+            pltpu.SMEM((16, 8), jnp.int32),
             pltpu.SemaphoreType.DMA((11,)),
             pltpu.SemaphoreType.DMA((len(NAMES),)),
             pltpu.SemaphoreType.DMA((len(NAMES),)),
@@ -403,23 +438,12 @@
         compiler_params=pltpu.CompilerParams(
             collective_id=0, has_side_effects=True, vmem_limit_bytes=60 * 2**20
         ),
-    )(slash, vert, place, which, q, k, v)
+    )(slash, vert, q, k, v)
 
 
 def shards(queries, keys, values, vertical, slash):
-    slab = lax.axis_index("seq")
-    ids = jnp.arange(256, dtype=jnp.int32)
-    flat = vertical.reshape(-1)
-    used = jnp.any(flat[:, None] == ids[None, :], axis=0)
-    earlier = used[None, :] & (ids[None, :] // 8 == flat[:, None] // 8) & (ids[None, :] < flat[:, None])
-    rank = jnp.sum(earlier.astype(jnp.int32), axis=1)
-    place = jnp.concatenate([vertical // 8, 2 * rank.reshape(8, 8)], axis=0)
-    mine = flat[:, None] - slab * 8
-    slots = jnp.arange(4, dtype=jnp.int32)[None, :]
-    hit = (mine >= 0) & (mine < 8) & (rank[:, None] == slots)
-    which = jnp.max(jnp.where(hit, mine, 0), axis=0, keepdims=True)
     return attention(
-        slash, vertical, place, which, queries, keys.reshape(8, BLK, BLK), values.reshape(8, BLK, BLK)
+        slash, vertical, queries, keys.reshape(8, BLK, BLK), values.reshape(8, BLK, BLK)
     )
 
 

time: 97.1 us -> 93.8 us (0.966)
  other arithmetic: 2.25 us -> 0 us
where the time goes in v6:
time: 93.8 us; the launch traced here: 93.4 us
  Pallas kernels  90.2 us (96%)
  local copies, waits for them, and re-layouts  3.13 us (3%)
    pallas_call x1, Pallas kernels, attention(): pl.pallas_call(kernel, out_shape=jax.ShapeDtypeStruct((256, 4096), BF16),...  90.2 us
    unnamed x1, local copies, waits for them, and re-layouts  3.13 us

profile of v6, /device:TPU:7, one launch (start us, length us, event | category | flops | bytes accessed | tf_op | source)
XLA Modules:
  0.0 93.4 jit_solution(2627467661217797408)
XLA Ops:
  0.0 90.2 %shard_map.55 = bf16[256,4096]{1,0:T(8,128)(2,1)} custom-call(s32[8,8]{1,0:T(8,128)} %slash.1, s32[8,8]{1,0:T(8,128)} %vert.1, bf16[1024,1024]{1,0:T(8,128)(2,1)} %q_hbm.1, bf16[8,128,128]{2,1,0:T(8,128)(2,1)} %bitcast.2, bf16[8,128,128]{2,1,0:T(8,128)(2,1)} %bitcast.3), custom_call_target="tpu_custom_call" | custom-call | tf_op jit(solution)/shard_map/pallas_call | solution.py:412
  90.3 3.1 %copy.7 = bf16[256,4096]{1,0:T(8,128)(2,1)} copy(bf16[256,4096]{1,0:T(8,128)(2,1)} %shard_map.55) | data formatting | bytes 4194304

commit v7 on v6

--- a/solution.py
+++ b/solution.py
@@ -371,7 +371,12 @@
     def keep(h):
         return pltpu.make_async_copy(quarter(h, 0), column(h), keep_sem.at[h])
 
-    far_put(0, 0, slab, slash, vert, place, q, far, stage, spots)
+    turn = 4 * (1 - group // 2)
+
+    def turned(e):
+        return (e // 8) * 8 + (e + turn) % 8
+
+    far_put(0, turned(0), slab, slash, vert, place, q, far, stage, spots)
 
     @pl.loop(0, 8)
     def _(h):
@@ -379,11 +384,11 @@
         def _(t):
             for u in range(FAR_STEPS):
                 e = h * 8 + t * FAR_STEPS + u
-                far_put((u + 1) % 2, jnp.minimum(e + 1, 63), slab, slash, vert, place, q, far, stage, spots)
-                far_finish(u % 2, e, far, acc, top, tot, out, stage, spots)
+                far_put((u + 1) % 2, turned(jnp.minimum(e + 1, 63)), slab, slash, vert, place, q, far, stage, spots)
+                far_finish(u % 2, turned(e), far, acc, top, tot, out, stage, spots)
             for n in (2, 1, 3):
-                pl.when(((group + n) % 4) // 2 == t)(lambda n=n: share(h, n).start())
-            pl.when(group // 2 == t)(lambda: keep(h).start())
+                pl.when((((group + n) % 4) // 2 + group // 2 + 1 + t) % 2 == 0)(lambda n=n: share(h, n).start())
+            pl.when(t == 1)(lambda: keep(h).start())
 
 
     for name in NAMES:

time: 93.8 us -> 93.6 us (level)
  no operation moved by 1% of the time
where the time goes in v7:
time: 93.6 us; the launch traced here: 93.4 us
  Pallas kernels  90.3 us (96%)
  local copies, waits for them, and re-layouts  3.13 us (3%)
    pallas_call x1, Pallas kernels, attention(): pl.pallas_call(kernel, out_shape=jax.ShapeDtypeStruct((256, 4096), BF16),...  90.3 us
    unnamed x1, local copies, waits for them, and re-layouts  3.13 us

profile of v7, /device:TPU:7, one launch (start us, length us, event | category | flops | bytes accessed | tf_op | source)
XLA Modules:
  0.0 93.4 jit_solution(8737201498061575294)
XLA Ops:
  0.0 90.3 %shard_map.55 = bf16[256,4096]{1,0:T(8,128)(2,1)} custom-call(s32[8,8]{1,0:T(8,128)} %slash.1, s32[8,8]{1,0:T(8,128)} %vert.1, bf16[1024,1024]{1,0:T(8,128)(2,1)} %q_hbm.1, bf16[8,128,128]{2,1,0:T(8,128)(2,1)} %bitcast.2, bf16[8,128,128]{2,1,0:T(8,128)(2,1)} %bitcast.3), custom_call_target="tpu_custom_call" | custom-call | tf_op jit(solution)/shard_map/pallas_call | solution.py:417
  90.3 3.1 %copy.7 = bf16[256,4096]{1,0:T(8,128)(2,1)} copy(bf16[256,4096]{1,0:T(8,128)(2,1)} %shard_map.55) | data formatting | bytes 4194304
